TPU v7x, 32 devices: a whole 2x2x4 slice. The times are simulated.
32 devices in a mesh: fsdp: 8 (over z, core), chan: 4 (over y, x).
Axes of the slice: x: 2, y: 2, z: 4, core: 2. Of those that a mesh axis runs over, the one named last changes fastest.
Arguments:
- in_master: float32 [4096, 2, 4096], P(('fsdp', 'chan')), may hold values from -0.09375 to 0.09375
- in_moment: float32 [4096, 2, 4096], P(('fsdp', 'chan')), may hold values from -1.8 to 1.8
- in_velocity: float32 [4096, 2, 4096], P(('fsdp', 'chan')), may hold values from 0.05 to 1
- in_grad: bfloat16 [4096, 2, 4096], P(('fsdp', 'chan')), may hold values from -6 to 6
- out_master: float32 [4096, 4096], P(('fsdp', 'chan')), may hold values from -0.09375 to 0.09375
- out_moment: float32 [4096, 4096], P(('fsdp', 'chan')), may hold values from -1.8 to 1.8
- out_velocity: float32 [4096, 4096], P(('fsdp', 'chan')), may hold values from 0.001 to 1
- out_grad: bfloat16 [4096, 4096], P(('fsdp', 'chan')), may hold values from -6 to 6
- embed_table: bfloat16 [65536, 4096], P('fsdp', 'chan'), may hold values from -18 to 18
- tokens: int32 [4, 1024], P(None, 'fsdp'), may hold values from 0 to 65535, as said below
- conv_state: bfloat16 [1024, 3, 4096], P('fsdp', None, 'chan'), may hold values from -6 to 6
- ssm_state: float32 [1024, 16, 4096], P('fsdp', None, 'chan'), may hold values from -6 to 6
- conv_weight: float32 [4, 4096], P(None, 'chan'), may hold values from -3 to 3
- conv_bias: float32 [4096], P('chan'), may hold values from -3 to 3
- x_proj_w: bfloat16 [288, 4096], P(None, 'chan'), may hold values from -0.09375 to 0.09375
- dt_proj_w: bfloat16 [4096, 256], P('chan'), may hold values from -0.375 to 0.375
- dt_bias: float32 [4096], P('chan'), may hold values from -4.5 to -2
- a_log: float32 [16, 4096], P(None, 'chan'), may hold values from 0 to 2.77
- d_skip: float32 [4096], P('chan'), may hold values from 0.5 to 2
Outputs:
- in_master_new: float32 [4096, 2, 4096], P(('fsdp', 'chan'))
- out_master_new: float32 [4096, 4096], P(('fsdp', 'chan'))
- block_out: bfloat16 [4, 1024, 4096], P(None, 'fsdp', 'chan')
- conv_state_new: bfloat16 [1024, 3, 4096], P('fsdp', None, 'chan')
- ssm_state_new: float32 [1024, 16, 4096], P('fsdp', None, 'chan')
Inputs may be any that keep to these rules, and one draw needn't show every extreme that they name: Split the ids into 8 equal consecutive vocabulary blocks and the sequences into 8 equal consecutive replicas; of one replica's 4 x 128 tokens at most 128 lie in any one block, and some block holds exactly 128 of them.
All inputs are finite; a program needn't handle non-finite values.
Results may differ from a plain program's by a relative error of at most 0.012.
Values may be sent and summed in bfloat16 or wider, within the bound.
A program may use at most 192 MiB of HBM per device.

v0:
```python
import math

import jax
import jax.numpy as jnp
from jax import lax
from jax.sharding import PartitionSpec as P

RANK = 256
NSTATE = 16


learn_rate = 0.01
beta_first = 0.8
beta_second = 0.95
adam_eps = 1e-08
weight_decay = 0.1
bias_first = 1.0 - math.pow(0.8, 10)
bias_second = 1.0 - math.pow(0.95, 10)
norm_eps = 1e-06


def adam_update(master, moment, velocity, grad):
    gradient = grad.astype(jnp.float32)
    moment = beta_first * moment + (1.0 - beta_first) * gradient
    velocity = beta_second * velocity + (1.0 - beta_second) * gradient * gradient
    update = moment / bias_first / (jnp.sqrt(velocity / bias_second) + adam_eps)
    return master - learn_rate * (update + weight_decay * master)


def reorder_rows(block, groups, replicas):
    width = block.shape[1]
    shaped = block.reshape(groups, replicas, -1, width)
    return jnp.transpose(shaped, (1, 0, 2, 3)).reshape(-1, width)


def per_device(
    in_master,
    in_moment,
    in_velocity,
    in_grad,
    out_master,
    out_moment,
    out_velocity,
    out_grad,
    embed_table,
    tokens,
    conv_state,
    ssm_state,
    conv_weight,
    conv_bias,
    x_proj_w,
    dt_proj_w,
    dt_bias,
    a_log,
    d_skip,
):
    in_new = adam_update(in_master, in_moment, in_velocity, in_grad)
    out_new = adam_update(out_master, out_moment, out_velocity, out_grad)
    pieces = (
        in_new[:, 0, :].astype(jnp.bfloat16),
        in_new[:, 1, :].astype(jnp.bfloat16),
        out_new.astype(jnp.bfloat16),
    )
    groups = lax.axis_size("chan")
    replicas = lax.axis_size("fsdp")
    stacked = (
        lax.all_gather(pieces[0], "fsdp", axis=0, tiled=True),
        lax.all_gather(pieces[1], "fsdp", axis=0, tiled=True),
        lax.all_gather(pieces[2], "fsdp", axis=0, tiled=True),
    )
    spread = (
        lax.all_to_all(stacked[0], "chan", split_axis=1, concat_axis=0, tiled=True),
        lax.all_to_all(stacked[1], "chan", split_axis=1, concat_axis=0, tiled=True),
        lax.all_to_all(stacked[2], "chan", split_axis=1, concat_axis=0, tiled=True),
    )
    relay_x = reorder_rows(spread[0], groups, replicas)
    relay_z = reorder_rows(spread[1], groups, replicas)
    relay_out = reorder_rows(spread[2], groups, replicas)
    vocab_rows = embed_table.shape[0]
    every_token = lax.all_gather(tokens, "fsdp", axis=1, tiled=True)
    offset = every_token - lax.axis_index("fsdp") * vocab_rows
    inside = jnp.logical_and(offset >= 0, offset < vocab_rows)
    picked = jnp.take(embed_table, jnp.clip(offset, 0, vocab_rows - 1), axis=0)
    picked = jnp.where(inside[:, :, None], picked, jnp.zeros((), jnp.bfloat16))
    found = (
        lax.psum_scatter(picked, "fsdp", scatter_dimension=1, tiled=True)
        .astype(jnp.float32)
        .astype(jnp.bfloat16)
    )
    inputs = lax.all_gather(found, "chan", axis=2, tiled=True)
    steps, rows, width = inputs.shape
    flat = inputs.reshape(steps * rows, width).astype(jnp.float32)
    normed = (flat * lax.rsqrt(jnp.mean(flat * flat, axis=1, keepdims=True) + norm_eps)).astype(
        jnp.bfloat16
    )
    x_in = (
        jnp.dot(normed, relay_x, preferred_element_type=jnp.float32)
        .astype(jnp.bfloat16)
        .reshape(steps, rows, -1)
    )
    z_in = (
        jnp.dot(normed, relay_z, preferred_element_type=jnp.float32)
        .astype(jnp.bfloat16)
        .reshape(steps, rows, -1)
    )
    decay = -jnp.exp(a_log)
    contract_last = (((1,), (1,)), ((), ()))
    window_state = conv_state
    state = ssm_state
    gates = []
    for step in range(steps):
        window = jnp.concatenate([window_state, x_in[step][:, None, :]], axis=1)
        mixed_conv = jnp.sum(window.astype(jnp.float32) * conv_weight[None], axis=1) + conv_bias
        act = jax.nn.silu(mixed_conv).astype(jnp.bfloat16)
        partial_value = lax.dot_general(
            act, x_proj_w, contract_last, preferred_element_type=jnp.float32
        )
        dbc = lax.psum(partial_value, "chan")
        dt_low = dbc[:, :RANK].astype(jnp.bfloat16)
        b_mat = dbc[:, RANK : RANK + NSTATE]
        c_mat = dbc[:, RANK + NSTATE :]
        delta = jax.nn.softplus(
            lax.dot_general(dt_low, dt_proj_w, contract_last, preferred_element_type=jnp.float32)
            + dt_bias
        )
        act_real = act.astype(jnp.float32)
        state = (
            jnp.exp(delta[:, None, :] * decay[None]) * state
            + (delta * act_real)[:, None, :] * b_mat[:, :, None]
        )
        y_out = jnp.sum(c_mat[:, :, None] * state, axis=1) + d_skip * act_real
        gated = (y_out * jax.nn.silu(z_in[step].astype(jnp.float32))).astype(jnp.bfloat16)
        gates.append(gated)
        window_state = window[:, 1:, :]
    stacked_gates = jnp.stack(gates)
    terms = lax.dot_general(
        stacked_gates, relay_out, (((2,), (1,)), ((), ())), preferred_element_type=jnp.float32
    )
    mixed_all = lax.psum_scatter(
        terms.astype(jnp.bfloat16), "chan", scatter_dimension=2, tiled=True
    ).astype(jnp.float32)
    block_out = (found.astype(jnp.float32) + mixed_all).astype(jnp.bfloat16)
    return (in_new, out_new, block_out, window_state, state)


def solution(mesh):
    placed = (
        P(("fsdp", "chan"), None, None),
        P(("fsdp", "chan"), None, None),
        P(("fsdp", "chan"), None, None),
        P(("fsdp", "chan"), None, None),
        P(("fsdp", "chan"), None),
        P(("fsdp", "chan"), None),
        P(("fsdp", "chan"), None),
        P(("fsdp", "chan"), None),
        P("fsdp", "chan"),
        P(None, "fsdp"),
        P("fsdp", None, "chan"),
        P("fsdp", None, "chan"),
        P(None, "chan"),
        P("chan"),
        P(None, "chan"),
        P("chan", None),
        P("chan"),
        P(None, "chan"),
        P("chan"),
    )
    return jax.shard_map(
        per_device,
        mesh=mesh,
        in_specs=placed,
        out_specs=(
            P(("fsdp", "chan"), None, None),
            P(("fsdp", "chan"), None),
            P(None, "fsdp", "chan"),
            P("fsdp", None, "chan"),
            P("fsdp", None, "chan"),
        ),
        check_vma=False,
    )
```

profile of v0, /device:TPU:0, one launch (start us, length us, event | category | flops | bytes accessed | tf_op | source)
XLA Modules:
  0.0 634.8 jit_solution(9839498305490577094)
XLA Ops:
  23.1 7.2 %copy.53 = f32[128,2,4096]{0,2,1:T(8,128)} copy(f32[128,2,4096]{2,1,0:T(2,128)} %param.19) | data formatting | bytes 8388608 | tf_op args[0]
  30.3 7.4 %copy.51 = f32[128,2,4096]{0,2,1:T(8,128)} copy(f32[128,2,4096]{2,1,0:T(2,128)} %param.21) | data formatting | bytes 8388608 | tf_op args[2]
  43.9 7.3 %copy.49 = f32[128,2,4096]{0,2,1:T(8,128)} copy(f32[128,2,4096]{2,1,0:T(2,128)} %param.20) | data formatting | bytes 8388608 | tf_op args[1]
  51.2 8.4 %fusion.63 = (bf16[128,2,4096]{0,2,1:T(8,128)(2,1)S(1)}, f32[128,2,4096]{0,2,1:T(8,128)}) fusion(f32[128,2,4096]{0,2,1:T(8,128)} %copy.53, f32[128,2,4096]{0,2,1:T(8,128)} %copy.51, bf16[128,2,4096]{0,2,1:T(8,128)(2,1)} %copy.50, f32[128,2,4096]{0,2,1:T(8,128)} %copy.49), kind=kLoop, calls=%fused_computation.141 | loop fusion | flops 17825792 | bytes 20971520 | tf_op jit(solution)/shard_map/convert.5
  61.9 25.0 %all_gather.15 = s32[4,1024]{1,0:T(4,128)S(1)} all-gather(s32[4,128]{1,0:T(4,128)S(1)} %copy-done.24), channel_id=1, replica_groups=mesh['fsdp'=8,'chan'=4] {'fsdp'}, dimensions={1}, use_global_device_ids=true | all-gather | bytes 18432 | tf_op jit(solution)/shard_map/all_gather | solution.py:80
  87.0 28.8 %gather_fusion = bf16[4096,1024]{1,0:T(8,128)(2,1)} fusion(bf16[8192,1024]{1,0:T(8,128)(2,1)} %param.27, s32[4096]{0:T(1024)S(1)} %bitcast_clamp_fusion), kind=kCustom, calls=%fused_computation | custom fusion | bytes 16793600 | tf_op jit(solution)/shard_map/jit(_take)/gather | solution.py:83
  115.8 7.9 %select_select_fusion = bf16[4,1024,1024]{2,1,0:T(8,128)(2,1)} fusion(bf16[4,1024,1024]{2,1,0:T(8,128)(2,1)} %bitcast.69, pred[4,1024]{1,0:T(4,128)(4,1)S(1)} %get-tuple-element.53, pred[4,1024]{1,0:T(4,128)(4,1)S(1)} %get-tuple-element.52), kind=kLoop, calls=%fused_computation.13 | loop fusion | flops 8388608 | bytes 16785408 | tf_op jit(solution)/shard_map/jit(_where)/select_n | solution.py:84
  129.4 62.1 %all-gather.13.cloned.1.call-done = bf16[1024,1,4096]{0,2,1:T(8,128)(2,1)} async-done(((bf16[128,1,4096]{0,2,1:T(8,128)(2,1)}), bf16[1024,1,4096]{0,2,1:T(8,128)(2,1)}) %all-gather.13.cloned.1.call-update) | async-done | bytes 8388624 | tf_op jit(solution)/shard_map/all_gather | solution.py:68
  191.4 31.0 %all-to-all-done.2 = bf16[1024,4,1024]{0,2,1:T(8,128)(2,1)} async-done(((bf16[1024,4,1024]{0,2,1:T(8,128)(2,1)}), bf16[1024,4,1024]{0,2,1:T(8,128)(2,1)}, u32[]{:S(2)}, u32[]{:S(2)}) %all-to-all-start.2) | async-done | bytes 8388640 | tf_op jit(solution)/shard_map/all_to_all | solution.py:74
  228.2 46.1 %all-gather.11.cloned.1.call-done = bf16[1024,1,4096]{0,2,1:T(8,128)(2,1)} async-done(((bf16[128,1,4096]{0,2,1:T(8,128)(2,1)}), bf16[1024,1,4096]{0,2,1:T(8,128)(2,1)}) %all-gather.11.cloned.1.call-update) | async-done | bytes 8388624 | tf_op jit(solution)/shard_map/all_gather | solution.py:67
  274.3 46.1 %all-to-all-done.1 = bf16[1024,4,1024]{0,2,1:T(8,128)(2,1)} async-done(((bf16[1024,4,1024]{0,2,1:T(8,128)(2,1)}), bf16[1024,4,1024]{0,2,1:T(8,128)(2,1)}, u32[]{:S(2)}, u32[]{:S(2)}) %all-to-all-start.1) | async-done | bytes 8388640 | tf_op jit(solution)/shard_map/all_to_all | solution.py:73
  326.3 38.5 %reduce-scatter.3.cloned.1.call-done = bf16[4,128,1024]{2,1,0:T(8,128)(2,1)} async-done(((bf16[4,1024,1024]{2,1,0:T(8,128)(2,1)}), bf16[4,128,1024]{2,1,0:T(8,128)(2,1)}) %reduce-scatter.3.cloned.1.call-update) | async-done | bytes 1048592 | tf_op jit(solution)/shard_map/reduce_scatter | solution.py:86
  365.0 11.6 %copy.69 = bf16[4,1024,1024]{2,1,0:T(8,128)(2,1)} copy(bf16[4,1024,1024]{1,2,0:T(8,128)(2,1)} %bitcast.19) | data formatting | bytes 16777216 | tf_op jit(solution)/shard_map/all_to_all | solution.py:74
  376.6 8.2 %copy.70 = bf16[8,4,128,1024]{3,2,1,0:T(8,128)(2,1)} copy(bf16[8,4,128,1024]{3,2,0,1:T(8,128)(2,1)} %bitcast.70) | data formatting | bytes 16777216 | tf_op jit(solution)/shard_map/transpose | solution.py:33
  384.9 8.9 %copy.75 = bf16[512,8,8,128]{3,2,1,0:T(8,128)(2,1)} copy(bf16[512,8,8,128]{3,1,2,0:T(8,128)(2,1)} %bitcast.38) | data formatting | bytes 16777216
  393.8 12.2 %copy.62 = bf16[4,8,128,1024]{3,2,0,1:T(8,128)(2,1)} copy(bf16[4,8,128,1024]{2,1,3,0:T(8,128)(2,1)} %bitcast.71) | data formatting | bytes 16777216 | tf_op jit(solution)/shard_map/reshape | solution.py:32
  406.0 23.4 %all-to-all-done = bf16[1024,4,1024]{0,2,1:T(8,128)(2,1)} async-done(((bf16[1024,4,1024]{0,2,1:T(8,128)(2,1)}), bf16[1024,4,1024]{0,2,1:T(8,128)(2,1)}, u32[]{:S(2)}, u32[]{:S(2)}) %all-to-all-start) | async-done | bytes 8388640 | tf_op jit(solution)/shard_map/all_to_all | solution.py:72
  429.3 9.2 %copy.74 = bf16[512,8,8,128]{3,2,1,0:T(8,128)(2,1)} copy(bf16[512,8,8,128]{3,1,2,0:T(8,128)(2,1)} %bitcast.32) | data formatting | bytes 16777216
  438.6 12.4 %copy.59 = bf16[4,8,128,1024]{3,2,0,1:T(8,128)(2,1)} copy(bf16[4,8,128,1024]{2,1,3,0:T(8,128)(2,1)} %bitcast.72) | data formatting | bytes 16777216 | tf_op jit(solution)/shard_map/reshape | solution.py:32
  477.6 10.2 %convolution_convert_fusion.1 = bf16[512,1024]{1,0:T(8,128)(2,1)} fusion(bf16[512,4096]{1,0:T(8,128)(2,1)} %bitcast.82, bf16[4096,1024]{1,0:T(8,128)(2,1)} %bitcast.79), kind=kOutput, calls=%fused_computation.48 | convolution fusion | flops 4295491584 | bytes 13631488 | tf_op jit(solution)/shard_map/dot_general | solution.py:102
  487.7 35.9 %all-reduce.3.cloned.1.call-done = (f32[128,288]{0,1:T(8,128)}, f32[128,288]{0,1:T(8,128)}, f32[128,288]{0,1:T(8,128)}, f32[128,288]{0,1:T(8,128)}) async-done(((f32[128,288]{0,1:T(8,128)}, f32[128,288]{0,1:T(8,128)}, f32[128,288]{0,1:T(8,128)}, f32[128,288]{0,1:T(8,128)}), (f32[128,288]{0,1:T(8,128)}, f32[128,288]{0,1:T(8,128)}, f32[128,288]{0,1:T(8,128)}, ...) | async-done | bytes 589840 | tf_op jit(solution)/shard_map/psum | solution.py:118
  546.1 17.0 %multiply_reduce_fusion.2 = (f32[128,1024]{1,0:T(8,128)S(1)}, f32[128,1024]{1,0:T(8,128)S(1)}, f32[128,1024]{1,0:T(8,128)S(1)}, f32[128,1024]{1,0:T(8,128)S(1)}, f32[128,16,1024]{2,1,0:T(8,128)}) fusion(f32[128,16]{1,0:T(8,128)} %copy.63, f32[128,16]{1,0:T(8,128)} %copy.64, f32[128,1024]{1,0:T(8,128)} %get-tuple-element.58, f32[128,16]{1,0:T(8,128)} %copy.61, ...), kind=kLoop, calls=%fused_computation.9 | loop fusion | flops 49807360 | bytes 23199744 | tf_op jit(solution)/shard_map/reduce_sum | solution.py:131
  571.8 7.2 %copy.71 = f32[128,2,4096]{2,1,0:T(2,128)} copy(f32[128,2,4096]{0,2,1:T(8,128)} %get-tuple-element.29) | data formatting | bytes 8388608
  582.7 41.8 %reduce-scatter.5.cloned.1.call-done = bf16[4,128,1024]{2,1,0:T(8,128)(2,1)} async-done(((bf16[4,128,4096]{2,1,0:T(8,128)(2,1)}), bf16[4,128,1024]{2,1,0:T(8,128)(2,1)}) %reduce-scatter.5.cloned.1.call-update) | async-done | bytes 1048592 | tf_op jit(solution)/shard_map/reduce_scatter | solution.py:139
  (118 shorter events, 106.0 us)
Async XLA Ops:
  7.2 466.1 %copy-start = (bf16[288,1024]{1,0:T(8,128)(2,1)S(1)}, bf16[288,1024]{1,0:T(8,128)(2,1)}, u32[]{:S(2)}) copy-start(bf16[288,1024]{1,0:T(8,128)(2,1)} %param.33) | copy-start | bytes 1769476
  7.2 116.5 %all-gather.9.cloned.1.call-start = ((), (), s32[]{:S(2)}) async-start(), calls=%async_computation.7 | async-start | bytes 9437184 | tf_op jit(solution)/shard_map/all_gather | solution.py:69
  23.1 168.3 %all-gather.13.cloned.1.call-start = ((), (), s32[]{:S(2)}) async-start(), calls=%async_computation.10 | async-start | bytes 9437184 | tf_op jit(solution)/shard_map/all_gather | solution.py:68
  61.1 213.2 %all-gather.11.cloned.1.call-start = ((), (), s32[]{:S(2)}) async-start(), calls=%async_computation.9 | async-start | bytes 9437184 | tf_op jit(solution)/shard_map/all_gather | solution.py:67
  61.9 302.9 %reduce-scatter.3.cloned.1.call-start = ((), (), s32[]{:S(2)}) async-start(), calls=%async_computation.5 | async-start | bytes 9437184 | tf_op jit(solution)/shard_map/reduce_scatter | solution.py:86
  123.7 98.7 %all-to-all-start.2 = ((bf16[1024,4,1024]{0,2,1:T(8,128)(2,1)}), bf16[1024,4,1024]{0,2,1:T(8,128)(2,1)}, u32[]{:S(2)}, u32[]{:S(2)}) async-start(bf16[1024,4,1024]{0,2,1:T(8,128)(2,1)} %bitcast.77), calls=%async_computation.3 | async-start | bytes 16777216 | tf_op jit(solution)/shard_map/all_to_all | solution.py:74
  222.5 97.9 %all-to-all-start.1 = ((bf16[1024,4,1024]{0,2,1:T(8,128)(2,1)}), bf16[1024,4,1024]{0,2,1:T(8,128)(2,1)}, u32[]{:S(2)}, u32[]{:S(2)}) async-start(bf16[1024,4,1024]{0,2,1:T(8,128)(2,1)} %bitcast.78), calls=%async_computation.2 | async-start | bytes 16777216 | tf_op jit(solution)/shard_map/all_to_all | solution.py:73
  320.4 44.6 %copy-start.20 = (f32[16,1024]{1,0:T(8,128)S(1)}, f32[16,1024]{1,0:T(8,128)}, u32[]{:S(2)}) copy-start(f32[16,1024]{1,0:T(8,128)} %param.36) | copy-start | bytes 196612
  320.4 108.9 %all-to-all-start = ((bf16[1024,4,1024]{0,2,1:T(8,128)(2,1)}), bf16[1024,4,1024]{0,2,1:T(8,128)(2,1)}, u32[]{:S(2)}, u32[]{:S(2)}) async-start(bf16[1024,4,1024]{0,2,1:T(8,128)(2,1)} %bitcast.76), calls=%async_computation.1 | async-start | bytes 16777216 | tf_op jit(solution)/shard_map/all_to_all | solution.py:72
  326.3 130.7 %all-gather.7.cloned.1.call-start = ((), (), s32[]{:S(2)}) async-start(), calls=%async_computation.6 | async-start | bytes 5242880 | tf_op jit(solution)/shard_map/all_gather | solution.py:90
  364.8 158.9 %all-reduce.3.cloned.1.call-start = ((), (), s32[]{:S(2)}) async-start(), calls=%async_computation.11 | async-start | bytes 1179648 | tf_op jit(solution)/shard_map/psum | solution.py:118
  461.9 7.9 %copy-start.6 = (bf16[4,128,4096]{2,1,0:T(8,128)(2,1)}, bf16[4,128,4096]{2,1,0:T(8,128)(2,1)S(1)}, u32[]{:S(2)}) copy-start(bf16[4,128,4096]{2,1,0:T(8,128)(2,1)S(1)} %fusion.1) | copy-start | bytes 12582916
  477.2 147.3 %reduce-scatter.5.cloned.1.call-start = ((), (), s32[]{:S(2)}) async-start(), calls=%async_computation.8 | async-start | bytes 5242880 | tf_op jit(solution)/shard_map/reduce_scatter | solution.py:139
  477.6 47.5 %copy-start.3 = (bf16[1024,256]{1,0:T(8,128)(2,1)S(1)}, bf16[1024,256]{1,0:T(8,128)(2,1)}, u32[]{:S(2)}) copy-start(bf16[1024,256]{1,0:T(8,128)(2,1)} %param.34) | copy-start | bytes 1572868
  477.6 47.5 %copy-start.19 = (f32[1024]{0:T(1024)S(1)}, f32[1024]{0:T(1024)}, u32[]{:S(2)}) copy-start(f32[1024]{0:T(1024)} %param.35) | copy-start | bytes 12292
  523.6 8.9 %copy-start.18 = (f32[128,288]{0,1:T(8,128)S(1)}, f32[128,288]{0,1:T(8,128)}, u32[]{:S(2)}) copy-start(f32[128,288]{0,1:T(8,128)} %get-tuple-element.22) | copy-start | bytes 442372
  523.6 10.3 %copy-start.12 = (bf16[128,1024]{1,0:T(8,128)(2,1)S(1)}, bf16[128,1024]{1,0:T(8,128)(2,1)}, u32[]{:S(2)}) copy-start(bf16[128,1024]{1,0:T(8,128)(2,1)} %copy-done.11) | copy-start | bytes 786436
  546.1 18.6 %slice-start = ((s8[8388608]{0:T(1024)(128)(4,1)}), s8[4194304]{0:T(1024)(128)(4,1)S(1)}, s32[]{:S(2)}) async-start(s8[8388608]{0:T(1024)(128)(4,1)} %bitcast.73), calls=%async_computation.12 | async-start | bytes 8388608
  546.1 17.0 %copy-start.8 = (bf16[128,1024]{1,0:T(8,128)(2,1)S(1)}, bf16[128,1024]{1,0:T(8,128)(2,1)}, u32[]{:S(2)}) copy-start(bf16[128,1024]{1,0:T(8,128)(2,1)} %copy-done.7) | copy-start | bytes 786436
  546.1 17.0 %copy-start.10 = (bf16[128,1024]{1,0:T(8,128)(2,1)S(1)}, bf16[128,1024]{1,0:T(8,128)(2,1)}, u32[]{:S(2)}) copy-start(bf16[128,1024]{1,0:T(8,128)(2,1)} %copy-done.9) | copy-start | bytes 786436
  546.1 17.1 %copy-start.13 = (bf16[128,1024]{1,0:T(8,128)(2,1)S(1)}, bf16[128,1024]{1,0:T(8,128)(2,1)}, u32[]{:S(2)}) copy-start(bf16[128,1024]{1,0:T(8,128)(2,1)} %copy-done.11) | copy-start | bytes 786436
  546.1 17.1 %copy-start.17 = (bf16[512,1024]{1,0:T(8,128)(2,1)S(1)}, bf16[512,1024]{1,0:T(8,128)(2,1)}, u32[]{:S(2)}) copy-start(bf16[512,1024]{1,0:T(8,128)(2,1)} %convolution_convert_fusion.1) | copy-start | bytes 3145732
  546.1 17.1 %copy-start.23 = (f32[1024]{0:T(1024)S(1)}, f32[1024]{0:T(1024)}, u32[]{:S(2)}) copy-start(f32[1024]{0:T(1024)} %param.37) | copy-start | bytes 12292
  546.1 18.6 %slice-start.1 = ((s8[8388608]{0:T(1024)(128)(4,1)}), s8[4194304]{0:T(1024)(128)(4,1)S(1)}, s32[]{:S(2)}) async-start(s8[8388608]{0:T(1024)(128)(4,1)} %bitcast.73), calls=%async_computation.13 | async-start | bytes 8388608
  (13 other events, 37.7 us)
Sparse Core Ops, SparseCore 0:
  23.2 85.2 all-gather.8
  110.7 80.6 all-gather.12
  193.6 80.6 all-gather.10
  277.0 87.6 reduce-scatter.2
  366.4 90.4 all-gather.6
  477.4 46.2 all-reduce.2
  571.9 52.5 reduce-scatter.4
where the time goes:
time: 645 us; the launch traced here: 635 us
  waiting for transfers between devices  332 us (51%)
  local copies, waits for them, and re-layouts  158 us (24%)
  other arithmetic  52.4 us (8%)
  matrix products  34.7 us (5%)
  blocking collectives  25 us (4%)
  starting transfers between devices  17.8 us (3%)
  between operations  15 us (2%)
    unnamed x66, local copies, waits for them, and re-layouts  70 us
    all_gather x1, waiting for transfers between devices, per_device(): lax.all_gather(pieces[1], 'fsdp', axis=0, tiled=True)  62.1 us
    all_gather x1, waiting for transfers between devices, per_device(): lax.all_gather(pieces[0], 'fsdp', axis=0, tiled=True)  46.1 us
    all_to_all x1, waiting for transfers between devices, per_device(): lax.all_to_all(stacked[1], 'chan', split_axis=1, concat_axis=0, tiled=True)  46.1 us
    reduce_scatter x1, waiting for transfers between devices, per_device(): lax.psum_scatter(terms.astype(jnp.bfloat16), 'chan', scatter_dimension=2,...  41.8 us
    reduce_scatter x1, waiting for transfers between devices, per_device(): lax.psum_scatter(picked, 'fsdp', scatter_dimension=1, tiled=True)  38.5 us
    psum x1, waiting for transfers between devices, per_device(): dbc = lax.psum(partial_value, 'chan')  35.9 us
    all_to_all x1, waiting for transfers between devices, per_device(): lax.all_to_all(stacked[2], 'chan', split_axis=1, concat_axis=0, tiled=True)  31 us
  transfers between devices with their start and end apart: 10, of which 9 were waited for; matrix products, arithmetic and copies ran while one was open for 25% of the time, Pallas kernels for 0%

commit v1 on v0

v1 whole, which is shorter than its diff:
```python
import math

import jax
import jax.numpy as jnp
from jax import lax
from jax.experimental.layout import Layout, with_layout_constraint
from jax.sharding import PartitionSpec as P

RANK = 256
NSTATE = 16


learn_rate = 0.01
beta_first = 0.8
beta_second = 0.95
adam_eps = 1e-08
weight_decay = 0.1
bias_first = 1.0 - math.pow(0.8, 10)
bias_second = 1.0 - math.pow(0.95, 10)
norm_eps = 1e-06


def adam_update(master, moment, velocity, grad):
    gradient = grad.astype(jnp.float32)
    moment = beta_first * moment + (1.0 - beta_first) * gradient
    velocity = beta_second * velocity + (1.0 - beta_second) * gradient * gradient
    update = moment / bias_first / (jnp.sqrt(velocity / bias_second) + adam_eps)
    return master - learn_rate * (update + weight_decay * master)


def row_major(block):
    return with_layout_constraint(block, Layout(tuple(range(block.ndim))))


def exchange(block, axis):
    return row_major(
        lax.all_to_all(row_major(block), axis, split_axis=0, concat_axis=0, tiled=True)
    )


def gather_by_exchange(block, axis):
    count = lax.axis_size(axis)
    spread = jnp.broadcast_to(block[None], (count,) + block.shape)
    return exchange(spread, axis)


def owned_rank(member):
    length = member.shape[0]
    earlier = lax.broadcasted_iota(jnp.int32, (length, length), 1) < lax.broadcasted_iota(
        jnp.int32, (length, length), 0
    )
    return jnp.dot(
        earlier.astype(jnp.bfloat16),
        member.astype(jnp.bfloat16),
        preferred_element_type=jnp.float32,
    ).astype(jnp.int32)


def find_inputs(embed_table, tokens):
    replicas = lax.axis_size("fsdp")
    vocab_rows = embed_table.shape[0]
    mine = tokens.reshape(-1)
    count = mine.shape[0]
    cap = 2 * count // replicas
    every = lax.all_gather(mine, "fsdp", axis=0, tiled=False)
    offset = every - lax.axis_index("fsdp") * vocab_rows
    inside = jnp.logical_and(offset >= 0, offset < vocab_rows)
    rank = owned_rank(inside.T).T
    key = jnp.where(inside, rank, -1)
    slot_ids = lax.broadcasted_iota(jnp.int32, (replicas, cap, count), 1)
    slots = jnp.sum(jnp.where(key[:, None, :] == slot_ids, offset[:, None, :], 0), axis=2)
    rows = embed_table.at[slots.reshape(-1)].get(mode="clip")
    got = exchange(rows, "fsdp")
    owner = mine // vocab_rows
    member = owner[:, None] == lax.broadcasted_iota(jnp.int32, (count, replicas), 1)
    place = owner * cap + jnp.sum(jnp.where(member, owned_rank(member), 0), axis=1)
    pick = place[:, None] == lax.broadcasted_iota(jnp.int32, (count, replicas * cap), 1)
    return jnp.dot(pick.astype(jnp.bfloat16), got, preferred_element_type=jnp.float32).astype(
        jnp.bfloat16
    )


def per_device(
    in_master,
    in_moment,
    in_velocity,
    in_grad,
    out_master,
    out_moment,
    out_velocity,
    out_grad,
    embed_table,
    tokens,
    conv_state,
    ssm_state,
    conv_weight,
    conv_bias,
    x_proj_w,
    dt_proj_w,
    dt_bias,
    a_log,
    d_skip,
):
    groups = lax.axis_size("chan")
    replicas = lax.axis_size("fsdp")
    steps, rows = tokens.shape
    in_new = adam_update(in_master, in_moment, in_velocity, in_grad)
    in_new = lax.optimization_barrier(row_major(in_new))
    out_new = adam_update(out_master, out_moment, out_velocity, out_grad)
    out_new = lax.optimization_barrier(row_major(out_new))
    x_piece = in_new[:, 0, :].astype(jnp.bfloat16)
    z_piece = in_new[:, 1, :].astype(jnp.bfloat16)
    out_piece = out_new.astype(jnp.bfloat16)

    def to_groups(piece):
        shaped = piece.reshape(piece.shape[0], groups, -1)
        split = jnp.transpose(shaped, (1, 0, 2))
        return exchange(split, "chan").reshape(-1, split.shape[2])

    x_own, z_own, out_own = to_groups(x_piece), to_groups(z_piece), to_groups(out_piece)
    relay_x = lax.all_gather(x_own, "fsdp", axis=0, tiled=True)
    relay_z = lax.all_gather(z_own, "fsdp", axis=0, tiled=True)
    half = out_own.shape[0] // 2
    relay_out = [
        lax.all_gather(out_own[at * half : (at + 1) * half], "fsdp", axis=0, tiled=True)
        for at in range(2)
    ]

    found = find_inputs(embed_table, tokens)
    parts = gather_by_exchange(found, "chan")
    flat = parts.astype(jnp.float32)
    width = groups * parts.shape[2]
    square = jnp.sum(jnp.sum(flat * flat, axis=2), axis=0) / width
    scale = lax.rsqrt(square + norm_eps)
    normed = (flat * scale[None, :, None]).astype(jnp.bfloat16)
    normed = jnp.transpose(normed, (1, 0, 2)).reshape(steps * rows, width)
    x_in = (
        jnp.dot(normed, relay_x, preferred_element_type=jnp.float32)
        .astype(jnp.bfloat16)
        .reshape(steps, rows, -1)
    )
    decay = -jnp.exp(a_log)
    contract_last = (((1,), (1,)), ((), ()))
    window = jnp.concatenate([jnp.transpose(conv_state, (1, 0, 2)), x_in], axis=0)
    taps = conv_weight.shape[0]
    acts = []
    for step in range(steps):
        total = conv_bias
        for tap in range(taps):
            total = total + window[step + tap].astype(jnp.float32) * conv_weight[tap]
        acts.append(jax.nn.silu(total).astype(jnp.bfloat16))
    act_all = jnp.concatenate(acts, axis=0)
    partial_value = lax.dot_general(
        act_all, x_proj_w, contract_last, preferred_element_type=jnp.float32
    )
    dbc = jnp.sum(gather_by_exchange(partial_value, "chan"), axis=0)
    delta_all = jax.nn.softplus(
        lax.dot_general(
            dbc[:, :RANK].astype(jnp.bfloat16),
            dt_proj_w,
            contract_last,
            preferred_element_type=jnp.float32,
        )
        + dt_bias
    ).reshape(steps, rows, -1)
    dbc = dbc.reshape(steps, rows, -1)
    state = ssm_state
    sums = []
    for step in range(steps):
        b_mat = dbc[step, :, RANK : RANK + NSTATE]
        c_mat = dbc[step, :, RANK + NSTATE :]
        delta = delta_all[step]
        act_real = acts[step].astype(jnp.float32)
        state = (
            jnp.exp(delta[:, None, :] * decay[None]) * state
            + (delta * act_real)[:, None, :] * b_mat[:, :, None]
        )
        sums.append(jnp.sum(c_mat[:, :, None] * state, axis=1) + d_skip * act_real)
    y_all = jnp.concatenate(sums, axis=0)
    z_in = jnp.dot(normed, relay_z, preferred_element_type=jnp.float32).astype(jnp.bfloat16)
    gated = (y_all * jax.nn.silu(z_in.astype(jnp.float32))).astype(jnp.bfloat16)
    mixed = []
    for part in relay_out:
        terms = jnp.stack(
            [
                lax.dot_general(
                    gated, block, contract_last, preferred_element_type=jnp.float32
                ).astype(jnp.bfloat16)
                for block in part.reshape(groups, -1, part.shape[1])
            ]
        )
        landed = exchange(terms, "chan")
        mixed.append(jnp.sum(landed.astype(jnp.float32), axis=0))
    blocks = [m.reshape(steps * rows, replicas // groups, half) for m in mixed]
    mixed_all = jnp.stack(blocks, axis=2).reshape(steps * rows, -1)
    block_out = (found.astype(jnp.float32) + mixed_all).astype(jnp.bfloat16)
    window_state = jnp.transpose(window[steps:], (1, 0, 2))
    return (in_new, out_new, block_out.reshape(steps, rows, -1), window_state, state)


def solution(mesh):
    placed = (
        P(("fsdp", "chan"), None, None),
        P(("fsdp", "chan"), None, None),
        P(("fsdp", "chan"), None, None),
        P(("fsdp", "chan"), None, None),
        P(("fsdp", "chan"), None),
        P(("fsdp", "chan"), None),
        P(("fsdp", "chan"), None),
        P(("fsdp", "chan"), None),
        P("fsdp", "chan"),
        P(None, "fsdp"),
        P("fsdp", None, "chan"),
        P("fsdp", None, "chan"),
        P(None, "chan"),
        P("chan"),
        P(None, "chan"),
        P("chan", None),
        P("chan"),
        P(None, "chan"),
        P("chan"),
    )
    return jax.shard_map(
        per_device,
        mesh=mesh,
        in_specs=placed,
        out_specs=(
            P(("fsdp", "chan"), None, None),
            P(("fsdp", "chan"), None),
            P(None, "fsdp", "chan"),
            P("fsdp", None, "chan"),
            P("fsdp", None, "chan"),
        ),
        check_vma=False,
    )
```

time: 645 us -> 466 us (0.72)
  waiting for transfers between devices: 332 us -> 203 us
  local copies, waits for them, and re-layouts: 158 us -> 58.6 us
  blocking collectives: 25 us -> 50.2 us
  other arithmetic: 52.4 us -> 65.5 us
  starting transfers between devices: 17.8 us -> 27.2 us
    all_gather x4, waiting for transfers between devices: 114 us -> 0.03 us  [the longest x2 0.02 us: per_device(): lax.all_gather(out_own[at * half:(at + 1) * half], 'fsdp', axis=0, tiled=...]
    all_to_all x3 -> x6, waiting for transfers between devices: 101 us -> 203 us  [exchange(): lax.all_to_all(row_major(block), axis, split_axis=0, concat_axis=0, tiled...]
    reduce_scatter x2 -> x0, waiting for transfers between devices: 80.3 us -> none  [the longest x1 41.8 us: per_device(): lax.psum_scatter(terms.astype(jnp.bfloat16), 'chan', scatter_dimension=2,...]
    unnamed x66 -> x37, local copies, waits for them, and re-layouts: 70 us -> 4.2 us
    all_to_all x0 -> x2, blocking collectives: none -> 36.6 us  [exchange(): lax.all_to_all(row_major(block), axis, split_axis=0, concat_axis=0, tiled...]
    psum x1 -> x0, waiting for transfers between devices: 35.9 us -> none  [per_device(): dbc = lax.psum(partial_value, 'chan')]
    reshape x2, local copies, waits for them, and re-layouts: 24.5 us -> 3.99 us  [the longest x1 2.68 us: per_device(): mixed_all = jnp.stack(blocks, axis=2).reshape(steps * rows, -1)]
    sub x0 -> x3, other arithmetic: none -> 19.7 us  [the longest x2 19.7 us: adam_update(): return master - learn_rate * (update + weight_decay * master)]
  transfers between devices with their start and end apart: 10 -> 10, of which waited for: 9 -> 5; matrix products, arithmetic and copies ran while one was open for 25% -> 25% of each run, Pallas kernels for 0% -> 0%
where the time goes in v1:
time: 466 us; the launch traced here: 457 us
  waiting for transfers between devices  203 us (44%)
  other arithmetic  65.5 us (14%)
  local copies, waits for them, and re-layouts  58.6 us (13%)
  blocking collectives  50.2 us (11%)
  matrix products  38.1 us (8%)
  starting transfers between devices  27.2 us (6%)
  between operations  14.7 us (3%)
    all_to_all x6, waiting for transfers between devices, exchange(): lax.all_to_all(row_major(block), axis, split_axis=0, concat_axis=0, tiled...  203 us
    all_to_all x2, blocking collectives, exchange(): lax.all_to_all(row_major(block), axis, split_axis=0, concat_axis=0, tiled...  36.6 us
    all_to_all x6, starting transfers between devices, exchange(): lax.all_to_all(row_major(block), axis, split_axis=0, concat_axis=0, tiled...  26.8 us
    sub x2, other arithmetic, adam_update(): return master - learn_rate * (update + weight_decay * master)  19.7 us
    reduce_sum x1, other arithmetic, per_device(): sums.append(jnp.sum(c_mat[:, :, None] * state, axis=1) + d_skip * act_real)  15.2 us
    gather x1, local copies, waits for them, and re-layouts, find_inputs(): rows = embed_table.at[slots.reshape(-1)].get(mode='clip')  14.1 us
    all_gather x1, blocking collectives, find_inputs(): every = lax.all_gather(mine, 'fsdp', axis=0, tiled=False)  13.6 us
    dot_general x8, matrix products, per_device(): lax.dot_general(gated, block, contract_last, preferred_element_type=jnp.f...  11.8 us
  transfers between devices with their start and end apart: 10, of which 5 were waited for; matrix products, arithmetic and copies ran while one was open for 25% of the time, Pallas kernels for 0%

profile of v1, /device:TPU:0, one launch (start us, length us, event | category | flops | bytes accessed | tf_op | source)
XLA Modules:
  0.0 457.3 jit_solution(7619600053801847597)
XLA Ops:
  7.2 15.2 %multiply_subtract_fusion = f32[128,2,4096]{2,1,0:T(2,128)S(1)} fusion(f32[128,2,4096]{2,1,0:T(2,128)} %param.19, f32[128,2,4096]{2,1,0:T(2,128)} %param.21, bf16[128,2,4096]{2,1,0:T(2,128)(2,1)} %param.22, f32[128,2,4096]{2,1,0:T(2,128)} %param.20), kind=kLoop, calls=%fused_computation.25 | loop fusion | flops 16777216 | bytes 18874368 | tf_op jit(solution)/shard_map/sub | solution.py:28
  24.5 5.6 %fusion.87 = (bf16[128,1,4096]{2,1,0:T(2,128)(2,1)S(1)}, bf16[128,1,4096]{2,1,0:T(2,128)(2,1)}) fusion(bf16[128,2,4096]{2,1,0:T(2,128)(2,1)S(1)} %convert.10), kind=kLoop, calls=%fused_computation.180 | loop fusion | bytes 4194304 | tf_op jit(solution)/shard_map/slice | solution.py:112
  30.1 5.4 %copy.58 = bf16[128,1,4096]{0,2,1:T(8,128)(2,1)} copy(bf16[128,1,4096]{2,1,0:T(2,128)(2,1)} %get-tuple-element.13) | data formatting | bytes 2097152 | tf_op jit(solution)/shard_map/slice | solution.py:111
  37.8 20.0 %all_to_all.47 = bf16[4,128,1024]{2,1,0:T(8,128)(2,1)} all-to-all(bf16[4,128,1024]{2,1,0:T(8,128)(2,1)} %bitcast.124), channel_id=1, replica_groups=mesh['fsdp'=8,'chan'=4] {'chan'}, dimensions={0} | all-to-all | bytes 2097152 | tf_op jit(solution)/shard_map/all_to_all | solution.py:37
  57.8 3.6 copy.63
  63.0 16.6 %all_to_all.48 = bf16[4,128,1024]{2,1,0:T(8,128)(2,1)} all-to-all(bf16[4,128,1024]{2,1,0:T(8,128)(2,1)S(1)} %bitcast.125), channel_id=1, replica_groups=mesh['fsdp'=8,'chan'=4] {'chan'}, dimensions={0} | all-to-all | bytes 2097152 | tf_op jit(solution)/shard_map/all_to_all | solution.py:37
  79.7 4.5 fusion.14
  91.2 13.6 %all-gather = s32[8,1,512]{2,1,0:T(1,128)S(1)} all-gather(s32[1,1,512]{2,1,0:T(1,128)S(1)} %bitcast.149), channel_id=1, replica_groups=mesh['fsdp'=8,'chan'=4] {'fsdp'}, dimensions={0}, use_global_device_ids=true | all-gather | bytes 18432 | tf_op jit(solution)/shard_map/all_gather | solution.py:65
  105.3 14.1 %gather_fusion = bf16[1024,1024]{1,0:T(8,128)(2,1)} fusion(bf16[8192,1024]{1,0:T(8,128)(2,1)} %param.27, s32[1024]{0:T(1024)S(1)} %broadcast_clamp_fusion), kind=kCustom, calls=%fused_computation | custom fusion | bytes 4198400 | tf_op jit(solution)/shard_map/gather | solution.py:72
  119.4 4.6 %all-to-all-start = ((bf16[8,128,1024]{2,1,0:T(8,128)(2,1)}), bf16[8,128,1024]{2,1,0:T(8,128)(2,1)}, u32[]{:S(2)}, u32[]{:S(2)}) async-start(bf16[8,128,1024]{2,1,0:T(8,128)(2,1)} %bitcast.5), calls=%async_computation | async-start | bytes 4194304 | tf_op jit(solution)/shard_map/all_to_all | solution.py:37
  125.5 91.4 %all-to-all-done = bf16[8,128,1024]{2,1,0:T(8,128)(2,1)} async-done(((bf16[8,128,1024]{2,1,0:T(8,128)(2,1)}), bf16[8,128,1024]{2,1,0:T(8,128)(2,1)}, u32[]{:S(2)}, u32[]{:S(2)}) %all-to-all-start) | async-done | bytes 2097184 | tf_op jit(solution)/shard_map/all_to_all | solution.py:37
  223.5 5.0 %all-to-all-start.1 = ((bf16[4,512,1024]{2,1,0:T(8,128)(2,1)}), bf16[4,512,1024]{2,1,0:T(8,128)(2,1)}, u32[]{:S(2)}, u32[]{:S(2)}) async-start(bf16[4,512,1024]{2,1,0:T(8,128)(2,1)} %broadcast_in_dim.28), calls=%async_computation.1 | async-start | bytes 8388608 | tf_op jit(solution)/shard_map/all_to_all | solution.py:37
  228.5 47.9 %all-to-all-done.1 = bf16[4,512,1024]{2,1,0:T(8,128)(2,1)} async-done(((bf16[4,512,1024]{2,1,0:T(8,128)(2,1)}), bf16[4,512,1024]{2,1,0:T(8,128)(2,1)}, u32[]{:S(2)}, u32[]{:S(2)}) %all-to-all-start.1) | async-done | bytes 4194336 | tf_op jit(solution)/shard_map/all_to_all | solution.py:37
  279.6 5.7 %fusion.8 = bf16[512,4,1024]{2,0,1:T(8,128)(2,1)} fusion(bf16[4,512,1024]{2,1,0:T(8,128)(2,1)} %all-to-all-done.1, f32[512]{0:T(512)S(1)} %add_rsqrt_fusion), kind=kLoop, calls=%fused_computation.22 | loop fusion | flops 6291456 | bytes 8390656 | tf_op jit(solution)/shard_map/transpose | solution.py:136
  285.3 6.3 %copy.57 = bf16[512,4,1024]{0,2,1:T(8,128)(2,1)} copy(bf16[512,4,1024]{2,0,1:T(8,128)(2,1)} %fusion.8) | data formatting | bytes 8388608 | tf_op jit(solution)/shard_map/transpose | solution.py:136
  291.5 9.3 %convolution_convert_fusion.1 = bf16[512,1024]{1,0:T(8,128)(2,1)S(1)} fusion(bf16[512,4096]{0,1:T(8,128)(2,1)} %bitcast.120, bf16[4096,1024]{1,0:T(8,128)(2,1)} %all-gather.6.cloned.1.call-done), kind=kOutput, calls=%fused_computation.54 | convolution fusion | flops 4295491584 | bytes 13631488 | tf_op jit(solution)/shard_map/dot_general | solution.py:138
  304.2 4.5 all-to-all-start.3
  309.4 26.7 %all-to-all-done.3 = f32[4,512,288]{1,2,0:T(8,128)} async-done(((f32[4,512,288]{1,2,0:T(8,128)}), f32[4,512,288]{1,2,0:T(8,128)}, u32[]{:S(2)}, u32[]{:S(2)}) %all-to-all-start.3) | async-done | bytes 2359328 | tf_op jit(solution)/shard_map/all_to_all | solution.py:37
  343.4 15.2 %multiply_reduce_fusion.2 = (f32[128,1024]{1,0:T(8,128)S(1)}, f32[128,1024]{1,0:T(8,128)S(1)}, f32[128,1024]{1,0:T(8,128)S(1)}, f32[128,1024]{1,0:T(8,128)S(1)}, f32[128,16,1024]{2,1,0:T(8,128)}) fusion(f32[128,16]{1,0:T(8,128)S(1)} %get-tuple-element.33, f32[128,16]{1,0:T(8,128)S(1)} %get-tuple-element.32, f32[128,1024]{1,0:T(8,128)S(1)} %get-tuple-element.16, ...), kind=kLoop, calls=%fused_computation.9 | loop fusion | flops 49807360 | bytes 23199744 | tf_op jit(solution)/shard_map/reduce_sum | solution.py:178
  360.1 10.6 %fusion.23 = bf16[512,1024]{1,0:T(8,128)(2,1)} fusion(f32[128,1024]{1,0:T(8,128)} %get-tuple-element.42, f32[128,1024]{1,0:T(8,128)} %get-tuple-element.41, f32[128,1024]{1,0:T(8,128)S(1)} %get-tuple-element.40, f32[128,1024]{1,0:T(8,128)S(1)} %get-tuple-element.39, bf16[512,4096]{0,1:T(8,128)(2,1)} %bitcast.121, ...), kind=kOutput, calls=%fused_computation.51 | convolution fusion | flops 4300734464 | bytes 15728640 | tf_op jit(solution)/shard_map/dot_general | solution.py:180
  378.6 4.7 %all-to-all-start.6 = ((bf16[4,512,512]{2,1,0:T(8,128)(2,1)}), bf16[4,512,512]{2,1,0:T(8,128)(2,1)}, u32[]{:S(2)}, u32[]{:S(2)}) async-start(bf16[4,512,512]{2,1,0:T(8,128)(2,1)} %pad_maximum_fusion), calls=%async_computation.6 | async-start | bytes 4194304 | tf_op jit(solution)/shard_map/all_to_all | solution.py:37
  390.5 17.3 %all-to-all-done.6 = bf16[4,512,512]{2,1,0:T(8,128)(2,1)} async-done(((bf16[4,512,512]{2,1,0:T(8,128)(2,1)}), bf16[4,512,512]{2,1,0:T(8,128)(2,1)}, u32[]{:S(2)}, u32[]{:S(2)}) %all-to-all-start.6) | async-done | bytes 2097184 | tf_op jit(solution)/shard_map/all_to_all | solution.py:37
  407.8 4.5 all-to-all-start.7
  417.4 19.3 %all-to-all-done.7 = bf16[4,512,512]{2,1,0:T(8,128)(2,1)} async-done(((bf16[4,512,512]{2,1,0:T(8,128)(2,1)}), bf16[4,512,512]{2,1,0:T(8,128)(2,1)}, u32[]{:S(2)}, u32[]{:S(2)}) %all-to-all-start.7) | async-done | bytes 2097184 | tf_op jit(solution)/shard_map/all_to_all | solution.py:37
  (100 shorter events, 71.0 us)
Async XLA Ops:
  7.2 294.8 %copy-start = (bf16[288,1024]{1,0:T(8,128)(2,1)S(1)}, bf16[288,1024]{1,0:T(8,128)(2,1)}, u32[]{:S(2)}) copy-start(bf16[288,1024]{1,0:T(8,128)(2,1)} %param.33) | copy-start | bytes 1769476
  7.2 284.3 %all-gather.6.cloned.1.call-start = ((), (), s32[]{:S(2)}) async-start(), calls=%async_computation.8 | async-start | bytes 9437184 | tf_op jit(solution)/shard_map/all_gather | solution.py:121
  22.4 7.7 %copy-start.2 = (f32[128,2,4096]{2,1,0:T(2,128)}, f32[128,2,4096]{2,1,0:T(2,128)S(1)}, u32[]{:S(2)}) copy-start(f32[128,2,4096]{2,1,0:T(2,128)S(1)} %multiply_subtract_fusion) | copy-start | bytes 12582916
  57.8 302.3 %all-gather.8.cloned.1.call-start = ((), (), s32[]{:S(2)}) async-start(), calls=%async_computation.9 | async-start | bytes 9437184 | tf_op jit(solution)/shard_map/all_gather | solution.py:122
  61.4 18.2 %copy-start.5 = (bf16[128,4096]{1,0:T(8,128)(2,1)S(1)}, bf16[128,4096]{1,0:T(8,128)(2,1)}, u32[]{:S(2)}) copy-start(bf16[128,4096]{1,0:T(8,128)(2,1)} %param.26) | copy-start | bytes 3145732
  85.5 5.6 %copy-start.9 = (s32[4,128]{1,0:T(4,128)S(1)}, s32[4,128]{1,0:T(4,128)}, u32[]{:S(2)}) copy-start(s32[4,128]{1,0:T(4,128)} %param.28) | copy-start | bytes 6148
  87.6 31.8 %all-to-all-start.5 = ((bf16[4,128,1024]{2,1,0:T(8,128)(2,1)}), bf16[4,128,1024]{2,1,0:T(8,128)(2,1)S(1)}, u32[]{:S(2)}, u32[]{:S(2)}) async-start(bf16[4,128,1024]{2,1,0:T(8,128)(2,1)} %bitcast.35), calls=%async_computation.5 | async-start | bytes 2097152 | tf_op jit(solution)/shard_map/all_to_all | solution.py:37
  119.4 97.5 %all-to-all-start = ((bf16[8,128,1024]{2,1,0:T(8,128)(2,1)}), bf16[8,128,1024]{2,1,0:T(8,128)(2,1)}, u32[]{:S(2)}, u32[]{:S(2)}) async-start(bf16[8,128,1024]{2,1,0:T(8,128)(2,1)} %bitcast.5), calls=%async_computation | async-start | bytes 4194304 | tf_op jit(solution)/shard_map/all_to_all | solution.py:37
  124.0 246.7 %all-gather.10.cloned.1.call-start = ((), (), s32[]{:S(2)}) async-start(), calls=%async_computation.10 | async-start | bytes 4718592 | tf_op jit(solution)/shard_map/all_gather | solution.py:125
  223.5 5.0 %copy-start.10 = (f32[4,1024]{1,0:T(4,128)S(1)}, f32[4,1024]{1,0:T(4,128)}, u32[]{:S(2)}) copy-start(f32[4,1024]{1,0:T(4,128)} %param.31) | copy-start | bytes 49156
  223.5 52.9 %all-to-all-start.1 = ((bf16[4,512,1024]{2,1,0:T(8,128)(2,1)}), bf16[4,512,1024]{2,1,0:T(8,128)(2,1)}, u32[]{:S(2)}, u32[]{:S(2)}) async-start(bf16[4,512,1024]{2,1,0:T(8,128)(2,1)} %broadcast_in_dim.28), calls=%async_computation.1 | async-start | bytes 8388608 | tf_op jit(solution)/shard_map/all_to_all | solution.py:37
  291.5 9.3 %copy-start.7 = (f32[1024]{0:T(1024)S(1)}, f32[1024]{0:T(1024)}, u32[]{:S(2)}) copy-start(f32[1024]{0:T(1024)} %param.32) | copy-start | bytes 12292
  291.5 9.6 %copy-start.6 = (bf16[128,3,1024]{2,0,1:T(8,128)(2,1)S(1)}, bf16[128,3,1024]{2,0,1:T(8,128)(2,1)}, u32[]{:S(2)}) copy-start(bf16[128,3,1024]{2,0,1:T(8,128)(2,1)} %param.29) | copy-start | bytes 2359300
  302.5 6.9 %copy-start.8 = (f32[16,1024]{1,0:T(8,128)S(1)}, f32[16,1024]{1,0:T(8,128)}, u32[]{:S(2)}) copy-start(f32[16,1024]{1,0:T(8,128)} %param.36) | copy-start | bytes 196612
  304.2 31.9 %all-to-all-start.3 = ((f32[4,512,288]{1,2,0:T(8,128)}), f32[4,512,288]{1,2,0:T(8,128)}, u32[]{:S(2)}, u32[]{:S(2)}) async-start(f32[4,512,288]{1,2,0:T(8,128)} %broadcast_in_dim.29.clone), calls=%async_computation.3 | async-start | bytes 4718592 | tf_op jit(solution)/shard_map/all_to_all | solution.py:37
  308.8 29.8 %copy-start.14 = (f32[1024]{0:T(1024)S(1)}, f32[1024]{0:T(1024)}, u32[]{:S(2)}) copy-start(f32[1024]{0:T(1024)} %param.35) | copy-start | bytes 12292
  308.8 74.5 %all-gather.12.cloned.1.call-start = ((), (), s32[]{:S(2)}) async-start(), calls=%async_computation.11 | async-start | bytes 4718592 | tf_op jit(solution)/shard_map/all_gather | solution.py:125
  343.4 15.2 %copy-start.11 = (f32[1024]{0:T(1024)S(1)}, f32[1024]{0:T(1024)}, u32[]{:S(2)}) copy-start(f32[1024]{0:T(1024)} %param.37) | copy-start | bytes 12292
  370.7 4.7 %copy-start.15 = (bf16[512,1024]{1,0:T(8,128)(2,1)S(1)}, bf16[512,1024]{1,0:T(8,128)(2,1)}, u32[]{:S(2)}) copy-start(bf16[512,1024]{1,0:T(8,128)(2,1)} %fusion.23) | copy-start | bytes 3145732
  370.7 4.7 %copy-start.12 = (bf16[2048,1024]{1,0:T(8,128)(2,1)S(1)}, bf16[2048,1024]{1,0:T(8,128)(2,1)}, u32[]{:S(2)}) copy-start(bf16[2048,1024]{1,0:T(8,128)(2,1)} %all-gather.10.cloned.1.call-done) | copy-start | bytes 12582916
  378.6 29.2 %all-to-all-start.6 = ((bf16[4,512,512]{2,1,0:T(8,128)(2,1)}), bf16[4,512,512]{2,1,0:T(8,128)(2,1)}, u32[]{:S(2)}, u32[]{:S(2)}) async-start(bf16[4,512,512]{2,1,0:T(8,128)(2,1)} %pad_maximum_fusion), calls=%async_computation.6 | async-start | bytes 4194304 | tf_op jit(solution)/shard_map/all_to_all | solution.py:37
  383.3 4.1 copy-start.13
  407.8 29.0 %all-to-all-start.7 = ((bf16[4,512,512]{2,1,0:T(8,128)(2,1)}), bf16[4,512,512]{2,1,0:T(8,128)(2,1)}, u32[]{:S(2)}, u32[]{:S(2)}) async-start(bf16[4,512,512]{2,1,0:T(8,128)(2,1)} %pad_maximum_fusion.1), calls=%async_computation.7 | async-start | bytes 4194304 | tf_op jit(solution)/shard_map/all_to_all | solution.py:37
  440.9 9.4 %copy-start.1 = (bf16[288,1024]{1,0:T(8,128)(2,1)S(1)}, bf16[288,1024]{1,0:T(8,128)(2,1)}, u32[]{:S(2)}) copy-start(bf16[288,1024]{1,0:T(8,128)(2,1)} %param.33) | copy-start | bytes 1769476
  (4 other events, 8.1 us)
Sparse Core Ops, SparseCore 0:
  57.9 92.1 all-gather.5
  151.7 100.7 all-gather.7
  254.1 45.2 all-gather.9
  310.9 45.9 all-gather.11

commit v2 on v1

--- a/solution.py
+++ b/solution.py
@@ -56,7 +56,7 @@
     ).astype(jnp.int32)
 
 
-def find_inputs(embed_table, tokens):
+def pick_rows(embed_table, tokens):
     replicas = lax.axis_size("fsdp")
     vocab_rows = embed_table.shape[0]
     mine = tokens.reshape(-1)
@@ -69,8 +69,15 @@
     key = jnp.where(inside, rank, -1)
     slot_ids = lax.broadcasted_iota(jnp.int32, (replicas, cap, count), 1)
     slots = jnp.sum(jnp.where(key[:, None, :] == slot_ids, offset[:, None, :], 0), axis=2)
-    rows = embed_table.at[slots.reshape(-1)].get(mode="clip")
-    got = exchange(rows, "fsdp")
+    return embed_table.at[slots.reshape(-1)].get(mode="clip")
+
+
+def find_inputs(embed_table, tokens, got):
+    replicas = lax.axis_size("fsdp")
+    vocab_rows = embed_table.shape[0]
+    mine = tokens.reshape(-1)
+    count = mine.shape[0]
+    cap = 2 * count // replicas
     owner = mine // vocab_rows
     member = owner[:, None] == lax.broadcasted_iota(jnp.int32, (count, replicas), 1)
     place = owner * cap + jnp.sum(jnp.where(member, owned_rank(member), 0), axis=1)
@@ -104,29 +111,41 @@
     groups = lax.axis_size("chan")
     replicas = lax.axis_size("fsdp")
     steps, rows = tokens.shape
+    out_new = adam_update(out_master, out_moment, out_velocity, out_grad)
+    out_new = lax.optimization_barrier(row_major(out_new))
+
+    def split_columns(piece):
+        wide = piece.shape[1] // groups
+        cuts = [piece[:, at * wide : (at + 1) * wide] for at in range(groups)]
+        return row_major(jnp.stack(cuts).astype(jnp.bfloat16))
+
+    def to_groups(split):
+        return exchange(split, "chan").reshape(-1, split.shape[2])
+
+    out_split = lax.optimization_barrier(split_columns(out_new))
+    out_own = to_groups(out_split)
+    tokens, out_own = lax.optimization_barrier((tokens, out_own))
+    rows_found = pick_rows(embed_table, tokens)
+    in_master, in_grad, rows_found = lax.optimization_barrier((in_master, in_grad, rows_found))
     in_new = adam_update(in_master, in_moment, in_velocity, in_grad)
     in_new = lax.optimization_barrier(row_major(in_new))
-    out_new = adam_update(out_master, out_moment, out_velocity, out_grad)
-    out_new = lax.optimization_barrier(row_major(out_new))
-    x_piece = in_new[:, 0, :].astype(jnp.bfloat16)
-    z_piece = in_new[:, 1, :].astype(jnp.bfloat16)
-    out_piece = out_new.astype(jnp.bfloat16)
-
-    def to_groups(piece):
-        shaped = piece.reshape(piece.shape[0], groups, -1)
-        split = jnp.transpose(shaped, (1, 0, 2))
-        return exchange(split, "chan").reshape(-1, split.shape[2])
-
-    x_own, z_own, out_own = to_groups(x_piece), to_groups(z_piece), to_groups(out_piece)
+    x_split = split_columns(in_new[:, 0, :])
+    z_split = split_columns(in_new[:, 1, :])
+    got = exchange(rows_found, "fsdp")
+    x_split, z_split, got = lax.optimization_barrier((x_split, z_split, got))
+    x_own = to_groups(x_split)
+    z_split, x_own = lax.optimization_barrier((z_split, x_own))
+    z_own = to_groups(z_split)
+    got, x_own, z_own = lax.optimization_barrier((got, x_own, z_own))
+    half = out_own.shape[0] // 2
+    relay_first = lax.all_gather(out_own[:half], "fsdp", axis=0, tiled=True)
+    x_own, z_own, relay_first = lax.optimization_barrier((x_own, z_own, relay_first))
     relay_x = lax.all_gather(x_own, "fsdp", axis=0, tiled=True)
     relay_z = lax.all_gather(z_own, "fsdp", axis=0, tiled=True)
-    half = out_own.shape[0] // 2
-    relay_out = [
-        lax.all_gather(out_own[at * half : (at + 1) * half], "fsdp", axis=0, tiled=True)
-        for at in range(2)
-    ]
-
-    found = find_inputs(embed_table, tokens)
+    out_rest, relay_x = lax.optimization_barrier((out_own[half:], relay_x))
+    relay_out = [relay_first, lax.all_gather(out_rest, "fsdp", axis=0, tiled=True)]
+
+    found = find_inputs(embed_table, tokens, got)
     parts = gather_by_exchange(found, "chan")
     flat = parts.astype(jnp.float32)
     width = groups * parts.shape[2]
@@ -191,8 +210,10 @@
         )
         landed = exchange(terms, "chan")
         mixed.append(jnp.sum(landed.astype(jnp.float32), axis=0))
-    blocks = [m.reshape(steps * rows, replicas // groups, half) for m in mixed]
-    mixed_all = jnp.stack(blocks, axis=2).reshape(steps * rows, -1)
+    cuts = [
+        m[:, at * half : (at + 1) * half] for at in range(replicas // groups) for m in mixed
+    ]
+    mixed_all = jnp.concatenate(cuts, axis=1)
     block_out = (found.astype(jnp.float32) + mixed_all).astype(jnp.bfloat16)
     window_state = jnp.transpose(window[steps:], (1, 0, 2))
     return (in_new, out_new, block_out.reshape(steps, rows, -1), window_state, state)

time: 466 us -> 445 us (0.955)
  local copies, waits for them, and re-layouts: 58.6 us -> 39.2 us
  waiting for transfers between devices: 203 us -> 217 us
  blocking collectives: 50.2 us -> 43.9 us
  other arithmetic: 65.5 us -> 59.9 us
    all_to_all x6, waiting for transfers between devices: 203 us -> 166 us  [exchange(): lax.all_to_all(row_major(block), axis, split_axis=0, concat_axis=0, tiled...]
    all_gather x2, waiting for transfers between devices: 0.02 us -> 27.4 us  [the longest x1 27.4 us: per_device(): lax.all_gather(out_rest, 'fsdp', axis=0, tiled=True)]
    all_gather x1, waiting for transfers between devices: 0.01 us -> 12.9 us  [per_device(): relay_x = lax.all_gather(x_own, 'fsdp', axis=0, tiled=True)]
    all_gather x1, waiting for transfers between devices: 0.01 us -> 10 us  [per_device(): relay_z = lax.all_gather(z_own, 'fsdp', axis=0, tiled=True)]
    slice x4, local copies, waits for them, and re-layouts: 15.6 us -> 5.74 us  [the longest x1 4.54 us: per_device(): z_split = split_columns(in_new[:, 1, :])]
    all_to_all x2, blocking collectives: 36.6 us -> 30.9 us  [exchange(): lax.all_to_all(row_major(block), axis, split_axis=0, concat_axis=0, tiled...]
  transfers between devices with their start and end apart: 10 -> 10, of which waited for: 5 -> 8; matrix products, arithmetic and copies ran while one was open for 25% -> 24% of each run, Pallas kernels for 0% -> 0%
where the time goes in v2:
time: 445 us; the launch traced here: 439 us
  waiting for transfers between devices  217 us (49%)
  other arithmetic  59.9 us (13%)
  blocking collectives  43.9 us (10%)
  local copies, waits for them, and re-layouts  39.2 us (9%)
  matrix products  35.2 us (8%)
  starting transfers between devices  29.5 us (7%)
  between operations  14.5 us (3%)
    all_to_all x6, waiting for transfers between devices, exchange(): lax.all_to_all(row_major(block), axis, split_axis=0, concat_axis=0, tiled...  166 us
    all_to_all x2, blocking collectives, exchange(): lax.all_to_all(row_major(block), axis, split_axis=0, concat_axis=0, tiled...  30.9 us
    all_to_all x6, starting transfers between devices, exchange(): lax.all_to_all(row_major(block), axis, split_axis=0, concat_axis=0, tiled...  28.6 us
    all_gather x1, waiting for transfers between devices, per_device(): lax.all_gather(out_rest, 'fsdp', axis=0, tiled=True)  27.4 us
    sub x2, other arithmetic, adam_update(): return master - learn_rate * (update + weight_decay * master)  20 us
    reduce_sum x1, other arithmetic, per_device(): sums.append(jnp.sum(c_mat[:, :, None] * state, axis=1) + d_skip * act_real)  15.2 us
    gather x1, local copies, waits for them, and re-layouts, pick_rows(): return embed_table.at[slots.reshape(-1)].get(mode='clip')  13.9 us
    all_gather x1, blocking collectives, pick_rows(): every = lax.all_gather(mine, 'fsdp', axis=0, tiled=False)  13 us
  transfers between devices with their start and end apart: 10, of which 8 were waited for; matrix products, arithmetic and copies ran while one was open for 24% of the time, Pallas kernels for 0%

profile of v2, /device:TPU:0, one launch (start us, length us, event | category | flops | bytes accessed | tf_op | source)
XLA Modules:
  0.0 439.3 jit_solution(1109739684501374166)
XLA Ops:
  7.2 4.9 %fusion.14 = f32[128,4096]{1,0:T(8,128)S(1)} fusion(f32[128,4096]{1,0:T(8,128)} %param.23, bf16[128,4096]{1,0:T(8,128)(2,1)} %param.26, f32[128,4096]{1,0:T(8,128)} %param.25, f32[128,4096]{1,0:T(8,128)} %param.24), kind=kLoop, calls=%fused_computation.35 | loop fusion | flops 8388608 | bytes 9437184 | tf_op jit(solution)/shard_map/sub | solution.py:28
  14.7 5.2 %all-to-all-start = ((bf16[4,128,1024]{2,1,0:T(8,128)(2,1)}), bf16[4,128,1024]{2,1,0:T(8,128)(2,1)S(1)}, u32[]{:S(2)}, u32[]{:S(2)}) async-start(bf16[4,128,1024]{2,1,0:T(8,128)(2,1)} %pad_maximum_fusion.2), calls=%async_computation | async-start | bytes 2097152 | tf_op jit(solution)/shard_map/all_to_all | solution.py:37
  19.9 13.6 %all-to-all-done = bf16[4,128,1024]{2,1,0:T(8,128)(2,1)S(1)} async-done(((bf16[4,128,1024]{2,1,0:T(8,128)(2,1)}), bf16[4,128,1024]{2,1,0:T(8,128)(2,1)S(1)}, u32[]{:S(2)}, u32[]{:S(2)}) %all-to-all-start) | async-done | bytes 1048608 | tf_op jit(solution)/shard_map/all_to_all | solution.py:37
  33.5 13.0 %all-gather = s32[8,1,512]{2,1,0:T(1,128)S(1)} all-gather(s32[1,1,512]{2,1,0:T(1,128)S(1)} %bitcast.164), channel_id=1, replica_groups=mesh['fsdp'=8,'chan'=4] {'fsdp'}, dimensions={0}, use_global_device_ids=true | all-gather | bytes 18432 | tf_op jit(solution)/shard_map/all_gather | solution.py:65
  47.1 13.9 %gather_fusion = bf16[1024,1024]{1,0:T(8,128)(2,1)} fusion(bf16[8192,1024]{1,0:T(8,128)(2,1)} %param.27, s32[1024]{0:T(1024)S(1)} %broadcast_clamp_fusion), kind=kCustom, calls=%fused_computation | custom fusion | bytes 4198400 | tf_op jit(solution)/shard_map/gather | solution.py:72
  67.1 15.2 %multiply_subtract_fusion = f32[128,2,4096]{2,1,0:T(2,128)S(1)} fusion(f32[128,2,4096]{2,1,0:T(2,128)} %param.19, f32[128,2,4096]{2,1,0:T(2,128)} %param.21, bf16[128,2,4096]{2,1,0:T(2,128)(2,1)} %param.22, f32[128,2,4096]{2,1,0:T(2,128)} %param.20), kind=kLoop, calls=%fused_computation.25 | loop fusion | flops 16777216 | bytes 18874368 | tf_op jit(solution)/shard_map/sub | solution.py:28
  82.3 4.5 %fusion.90 = (bf16[128,1,4096]{2,1,0:T(2,128)(2,1)S(1)}, bf16[128,1,4096]{2,1,0:T(2,128)(2,1)S(1)}) fusion(f32[128,2,4096]{2,1,0:T(2,128)S(1)} %multiply_subtract_fusion), kind=kLoop, calls=%fused_computation.199 | loop fusion | bytes 4194304 | tf_op jit(solution)/shard_map/slice | solution.py:133
  89.7 58.4 %all-to-all-done.1 = bf16[8,128,1024]{2,1,0:T(8,128)(2,1)} async-done(((bf16[8,128,1024]{2,1,0:T(8,128)(2,1)}), bf16[8,128,1024]{2,1,0:T(8,128)(2,1)}, u32[]{:S(2)}, u32[]{:S(2)}) %all-to-all-start.1) | async-done | bytes 2097184 | tf_op jit(solution)/shard_map/all_to_all | solution.py:37
  148.1 16.1 %all_to_all.47 = bf16[4,128,1024]{2,1,0:T(8,128)(2,1)} all-to-all(bf16[4,128,1024]{2,1,0:T(8,128)(2,1)S(1)} %pad_maximum_fusion.3), channel_id=1, replica_groups=mesh['fsdp'=8,'chan'=4] {'chan'}, dimensions={0} | all-to-all | bytes 2097152 | tf_op jit(solution)/shard_map/all_to_all | solution.py:37
  164.2 14.7 %all_to_all.48 = bf16[4,128,1024]{2,1,0:T(8,128)(2,1)} all-to-all(bf16[4,128,1024]{2,1,0:T(8,128)(2,1)S(1)} %pad_maximum_fusion.4), channel_id=1, replica_groups=mesh['fsdp'=8,'chan'=4] {'chan'}, dimensions={0} | all-to-all | bytes 2097152 | tf_op jit(solution)/shard_map/all_to_all | solution.py:37
  185.5 5.3 %all-to-all-start.4 = ((bf16[4,512,1024]{2,1,0:T(8,128)(2,1)}), bf16[4,512,1024]{2,1,0:T(8,128)(2,1)}, u32[]{:S(2)}, u32[]{:S(2)}) async-start(bf16[4,512,1024]{2,1,0:T(8,128)(2,1)} %broadcast_in_dim.28), calls=%async_computation.4 | async-start | bytes 8388608 | tf_op jit(solution)/shard_map/all_to_all | solution.py:37
  190.8 43.3 %all-to-all-done.4 = bf16[4,512,1024]{2,1,0:T(8,128)(2,1)} async-done(((bf16[4,512,1024]{2,1,0:T(8,128)(2,1)}), bf16[4,512,1024]{2,1,0:T(8,128)(2,1)}, u32[]{:S(2)}, u32[]{:S(2)}) %all-to-all-start.4) | async-done | bytes 4194336 | tf_op jit(solution)/shard_map/all_to_all | solution.py:37
  237.3 5.7 %fusion.8 = bf16[512,4,1024]{2,0,1:T(8,128)(2,1)} fusion(bf16[4,512,1024]{2,1,0:T(8,128)(2,1)} %all-to-all-done.4, f32[512]{0:T(512)S(1)} %add_rsqrt_fusion), kind=kLoop, calls=%fused_computation.22 | loop fusion | flops 6291456 | bytes 8390656 | tf_op jit(solution)/shard_map/transpose | solution.py:155
  242.9 6.3 %copy.41 = bf16[512,4,1024]{0,2,1:T(8,128)(2,1)} copy(bf16[512,4,1024]{2,0,1:T(8,128)(2,1)} %fusion.8) | data formatting | bytes 8388608 | tf_op jit(solution)/shard_map/transpose | solution.py:155
  249.2 12.9 %all-gather.8.cloned.1.call-done = bf16[4096,1024]{1,0:T(8,128)(2,1)} async-done(((bf16[512,1024]{1,0:T(8,128)(2,1)}), bf16[4096,1024]{1,0:T(8,128)(2,1)}) %all-gather.8.cloned.1.call-update) | async-done | bytes 8388624 | tf_op jit(solution)/shard_map/all_gather | solution.py:143
  262.1 9.2 %convolution_convert_fusion.1 = bf16[512,1024]{1,0:T(8,128)(2,1)S(1)} fusion(bf16[512,4096]{0,1:T(8,128)(2,1)} %bitcast.139, bf16[4096,1024]{1,0:T(8,128)(2,1)} %all-gather.8.cloned.1.call-done), kind=kOutput, calls=%fused_computation.56 | convolution fusion | flops 4295491584 | bytes 13631488 | tf_op jit(solution)/shard_map/dot_general | solution.py:157
  274.8 4.6 %all-to-all-start.5 = ((f32[4,512,288]{1,2,0:T(8,128)}), f32[4,512,288]{1,2,0:T(8,128)}, u32[]{:S(2)}, u32[]{:S(2)}) async-start(f32[4,512,288]{1,2,0:T(8,128)} %broadcast_in_dim.29.clone), calls=%async_computation.5 | async-start | bytes 4718592 | tf_op jit(solution)/shard_map/all_to_all | solution.py:37
  280.0 27.8 %all-to-all-done.5 = f32[4,512,288]{1,2,0:T(8,128)} async-done(((f32[4,512,288]{1,2,0:T(8,128)}), f32[4,512,288]{1,2,0:T(8,128)}, u32[]{:S(2)}, u32[]{:S(2)}) %all-to-all-start.5) | async-done | bytes 2359328 | tf_op jit(solution)/shard_map/all_to_all | solution.py:37
  317.4 15.2 %multiply_reduce_fusion.2 = (f32[128,1024]{1,0:T(8,128)S(1)}, f32[128,1024]{1,0:T(8,128)S(1)}, f32[128,1024]{1,0:T(8,128)S(1)}, f32[128,1024]{1,0:T(8,128)S(1)}, f32[128,16,1024]{2,1,0:T(8,128)}) fusion(f32[128,16]{1,0:T(8,128)S(1)} %get-tuple-element.85, f32[128,16]{1,0:T(8,128)S(1)} %get-tuple-element.84, f32[128,1024]{1,0:T(8,128)S(1)} %get-tuple-element.52, ...), kind=kLoop, calls=%fused_computation.9 | loop fusion | flops 49807360 | bytes 23199744 | tf_op jit(solution)/shard_map/reduce_sum | solution.py:197
  334.3 10.0 %all-gather.10.cloned.1.call-done = bf16[4096,1024]{1,0:T(8,128)(2,1)} async-done(((bf16[512,1024]{1,0:T(8,128)(2,1)}), bf16[4096,1024]{1,0:T(8,128)(2,1)}) %all-gather.10.cloned.1.call-update) | async-done | bytes 8388624 | tf_op jit(solution)/shard_map/all_gather | solution.py:144
  344.3 10.1 %fusion.24 = bf16[512,1024]{1,0:T(8,128)(2,1)S(1)} fusion(f32[128,1024]{1,0:T(8,128)} %get-tuple-element.94, f32[128,1024]{1,0:T(8,128)} %get-tuple-element.93, f32[128,1024]{1,0:T(8,128)} %get-tuple-element.92, f32[128,1024]{1,0:T(8,128)} %get-tuple-element.91, bf16[512,4096]{0,1:T(8,128)(2,1)} %bitcast.140, ...), kind=kOutput, calls=%fused_computation.53 | convolution fusion | flops 4300734464 | bytes 15728640 | tf_op jit(solution)/shard_map/dot_general | solution.py:199
  359.0 4.7 %all-to-all-start.6 = ((bf16[4,512,512]{2,1,0:T(8,128)(2,1)}), bf16[4,512,512]{2,1,0:T(8,128)(2,1)}, u32[]{:S(2)}, u32[]{:S(2)}) async-start(bf16[4,512,512]{2,1,0:T(8,128)(2,1)} %pad_maximum_fusion), calls=%async_computation.6 | async-start | bytes 4194304 | tf_op jit(solution)/shard_map/all_to_all | solution.py:37
  363.7 27.4 %all-gather.12.cloned.1.call-done = bf16[2048,1024]{1,0:T(8,128)(2,1)} async-done(((bf16[256,1024]{1,0:T(8,128)(2,1)}), bf16[2048,1024]{1,0:T(8,128)(2,1)}) %all-gather.12.cloned.1.call-update) | async-done | bytes 4194320 | tf_op jit(solution)/shard_map/all_gather | solution.py:146
  406.5 22.6 %all-to-all-done.7 = bf16[4,512,512]{2,1,0:T(8,128)(2,1)} async-done(((bf16[4,512,512]{2,1,0:T(8,128)(2,1)}), bf16[4,512,512]{2,1,0:T(8,128)(2,1)}, u32[]{:S(2)}, u32[]{:S(2)}) %all-to-all-start.7) | async-done | bytes 2097184 | tf_op jit(solution)/shard_map/all_to_all | solution.py:37
  (96 shorter events, 60.1 us)
Async XLA Ops:
  7.2 265.4 %copy-start = (bf16[288,1024]{1,0:T(8,128)(2,1)S(1)}, bf16[288,1024]{1,0:T(8,128)(2,1)}, u32[]{:S(2)}) copy-start(bf16[288,1024]{1,0:T(8,128)(2,1)} %param.33) | copy-start | bytes 1769476
  13.4 20.2 %copy-start.8 = (s32[4,128]{1,0:T(4,128)S(1)}, s32[4,128]{1,0:T(4,128)}, u32[]{:S(2)}) copy-start(s32[4,128]{1,0:T(4,128)} %param.28) | copy-start | bytes 6148
  14.7 18.8 %all-to-all-start = ((bf16[4,128,1024]{2,1,0:T(8,128)(2,1)}), bf16[4,128,1024]{2,1,0:T(8,128)(2,1)S(1)}, u32[]{:S(2)}, u32[]{:S(2)}) async-start(bf16[4,128,1024]{2,1,0:T(8,128)(2,1)} %pad_maximum_fusion.2), calls=%async_computation | async-start | bytes 2097152 | tf_op jit(solution)/shard_map/all_to_all | solution.py:37
  61.1 87.0 %all-to-all-start.1 = ((bf16[8,128,1024]{2,1,0:T(8,128)(2,1)}), bf16[8,128,1024]{2,1,0:T(8,128)(2,1)}, u32[]{:S(2)}, u32[]{:S(2)}) async-start(bf16[8,128,1024]{2,1,0:T(8,128)(2,1)} %bitcast.20), calls=%async_computation.1 | async-start | bytes 4194304 | tf_op jit(solution)/shard_map/all_to_all | solution.py:37
  65.4 113.5 %all-gather.6.cloned.1.call-start = ((), (), s32[]{:S(2)}) async-start(), calls=%async_computation.8 | async-start | bytes 4718592 | tf_op jit(solution)/shard_map/all_gather | solution.py:141
  66.6 195.6 %all-gather.8.cloned.1.call-start = ((), (), s32[]{:S(2)}) async-start(), calls=%async_computation.9 | async-start | bytes 9437184 | tf_op jit(solution)/shard_map/all_gather | solution.py:143
  82.3 4.6 %copy-start.2 = (f32[128,2,4096]{2,1,0:T(2,128)}, f32[128,2,4096]{2,1,0:T(2,128)S(1)}, u32[]{:S(2)}) copy-start(f32[128,2,4096]{2,1,0:T(2,128)S(1)} %multiply_subtract_fusion) | copy-start | bytes 12582916
  179.0 165.3 %all-gather.10.cloned.1.call-start = ((), (), s32[]{:S(2)}) async-start(), calls=%async_computation.10 | async-start | bytes 9437184 | tf_op jit(solution)/shard_map/all_gather | solution.py:144
  185.5 5.3 %copy-start.9 = (f32[4,1024]{1,0:T(4,128)S(1)}, f32[4,1024]{1,0:T(4,128)}, u32[]{:S(2)}) copy-start(f32[4,1024]{1,0:T(4,128)} %param.31) | copy-start | bytes 49156
  185.5 48.6 %all-to-all-start.4 = ((bf16[4,512,1024]{2,1,0:T(8,128)(2,1)}), bf16[4,512,1024]{2,1,0:T(8,128)(2,1)}, u32[]{:S(2)}, u32[]{:S(2)}) async-start(bf16[4,512,1024]{2,1,0:T(8,128)(2,1)} %broadcast_in_dim.28), calls=%async_computation.4 | async-start | bytes 8388608 | tf_op jit(solution)/shard_map/all_to_all | solution.py:37
  262.1 9.2 %copy-start.5 = (f32[1024]{0:T(1024)S(1)}, f32[1024]{0:T(1024)}, u32[]{:S(2)}) copy-start(f32[1024]{0:T(1024)} %param.32) | copy-start | bytes 12292
  262.1 9.6 %copy-start.4 = (bf16[128,3,1024]{2,0,1:T(8,128)(2,1)S(1)}, bf16[128,3,1024]{2,0,1:T(8,128)(2,1)}, u32[]{:S(2)}) copy-start(bf16[128,3,1024]{2,0,1:T(8,128)(2,1)} %param.29) | copy-start | bytes 2359300
  273.0 6.9 %copy-start.7 = (f32[16,1024]{1,0:T(8,128)S(1)}, f32[16,1024]{1,0:T(8,128)}, u32[]{:S(2)}) copy-start(f32[16,1024]{1,0:T(8,128)} %param.36) | copy-start | bytes 196612
  274.8 33.0 %all-to-all-start.5 = ((f32[4,512,288]{1,2,0:T(8,128)}), f32[4,512,288]{1,2,0:T(8,128)}, u32[]{:S(2)}, u32[]{:S(2)}) async-start(f32[4,512,288]{1,2,0:T(8,128)} %broadcast_in_dim.29.clone), calls=%async_computation.5 | async-start | bytes 4718592 | tf_op jit(solution)/shard_map/all_to_all | solution.py:37
  279.3 111.8 %all-gather.12.cloned.1.call-start = ((), (), s32[]{:S(2)}) async-start(), calls=%async_computation.11 | async-start | bytes 4718592 | tf_op jit(solution)/shard_map/all_gather | solution.py:146
  310.9 4.2 copy-start.6
  310.9 5.0 %slice-start = ((s8[8388608]{0:T(1024)(128)(4,1)}), s8[4194304]{0:T(1024)(128)(4,1)S(1)}, s32[]{:S(2)}) async-start(s8[8388608]{0:T(1024)(128)(4,1)} %bitcast.137), calls=%async_computation.12 | async-start | bytes 8388608
  317.4 15.2 %copy-start.10 = (f32[1024]{0:T(1024)S(1)}, f32[1024]{0:T(1024)}, u32[]{:S(2)}) copy-start(f32[1024]{0:T(1024)} %param.37) | copy-start | bytes 12292
  344.3 10.1 %copy-start.11 = (bf16[2048,1024]{1,0:T(8,128)(2,1)S(1)}, bf16[2048,1024]{1,0:T(8,128)(2,1)}, u32[]{:S(2)}) copy-start(bf16[2048,1024]{1,0:T(8,128)(2,1)} %all-gather.6.cloned.1.call-done) | copy-start | bytes 12582916
  359.0 40.0 %all-to-all-start.6 = ((bf16[4,512,512]{2,1,0:T(8,128)(2,1)}), bf16[4,512,512]{2,1,0:T(8,128)(2,1)}, u32[]{:S(2)}, u32[]{:S(2)}) async-start(bf16[4,512,512]{2,1,0:T(8,128)(2,1)} %pad_maximum_fusion), calls=%async_computation.6 | async-start | bytes 4194304 | tf_op jit(solution)/shard_map/all_to_all | solution.py:37
  391.1 4.7 %copy-start.12 = (bf16[2048,1024]{1,0:T(8,128)(2,1)S(1)}, bf16[2048,1024]{1,0:T(8,128)(2,1)}, u32[]{:S(2)}) copy-start(bf16[2048,1024]{1,0:T(8,128)(2,1)} %all-gather.12.cloned.1.call-done) | copy-start | bytes 12582916
  391.1 4.7 %copy-start.14 = (bf16[512,1024]{1,0:T(8,128)(2,1)S(1)}, bf16[512,1024]{1,0:T(8,128)(2,1)}, u32[]{:S(2)}) copy-start(bf16[512,1024]{1,0:T(8,128)(2,1)} %copy-done.13) | copy-start | bytes 3145732
  399.0 30.1 %all-to-all-start.7 = ((bf16[4,512,512]{2,1,0:T(8,128)(2,1)}), bf16[4,512,512]{2,1,0:T(8,128)(2,1)}, u32[]{:S(2)}, u32[]{:S(2)}) async-start(bf16[4,512,512]{2,1,0:T(8,128)(2,1)} %pad_maximum_fusion.1), calls=%async_computation.7 | async-start | bytes 4194304 | tf_op jit(solution)/shard_map/all_to_all | solution.py:37
  406.4 26.0 %copy-start.1 = (bf16[288,1024]{1,0:T(8,128)(2,1)S(1)}, bf16[288,1024]{1,0:T(8,128)(2,1)}, u32[]{:S(2)}) copy-start(bf16[288,1024]{1,0:T(8,128)(2,1)} %param.33) | copy-start | bytes 1769476
  (3 other events, 5.8 us)
Sparse Core Ops, SparseCore 0:
  68.4 81.1 all-gather.5
  179.1 82.9 all-gather.7
  263.7 80.5 all-gather.9
  345.8 45.3 all-gather.11

commit v3 on v2

--- a/solution.py
+++ b/solution.py
@@ -132,15 +132,13 @@
     x_split = split_columns(in_new[:, 0, :])
     z_split = split_columns(in_new[:, 1, :])
     got = exchange(rows_found, "fsdp")
-    x_split, z_split, got = lax.optimization_barrier((x_split, z_split, got))
     x_own = to_groups(x_split)
-    z_split, x_own = lax.optimization_barrier((z_split, x_own))
-    z_own = to_groups(z_split)
-    got, x_own, z_own = lax.optimization_barrier((got, x_own, z_own))
     half = out_own.shape[0] // 2
     relay_first = lax.all_gather(out_own[:half], "fsdp", axis=0, tiled=True)
-    x_own, z_own, relay_first = lax.optimization_barrier((x_own, z_own, relay_first))
+    z_split, relay_first, x_own = lax.optimization_barrier((z_split, relay_first, x_own))
     relay_x = lax.all_gather(x_own, "fsdp", axis=0, tiled=True)
+    z_own = to_groups(z_split)
+    got, z_own = lax.optimization_barrier((got, z_own))
     relay_z = lax.all_gather(z_own, "fsdp", axis=0, tiled=True)
     out_rest, relay_x = lax.optimization_barrier((out_own[half:], relay_x))
     relay_out = [relay_first, lax.all_gather(out_rest, "fsdp", axis=0, tiled=True)]

time: 445 us -> 455 us (1.022)
  blocking collectives: 43.9 us -> 135 us
  waiting for transfers between devices: 217 us -> 136 us
    all_to_all x2, blocking collectives: 30.9 us -> 121 us  [exchange(): lax.all_to_all(row_major(block), axis, split_axis=0, concat_axis=0, tiled...]
    all_to_all x6, waiting for transfers between devices: 166 us -> 136 us  [exchange(): lax.all_to_all(row_major(block), axis, split_axis=0, concat_axis=0, tiled...]
    all_gather x1, waiting for transfers between devices: 27.4 us -> 0.02 us  [per_device(): lax.all_gather(out_rest, 'fsdp', axis=0, tiled=True)]
    all_gather x1, waiting for transfers between devices: 12.9 us -> 0.01 us  [per_device(): relay_x = lax.all_gather(x_own, 'fsdp', axis=0, tiled=True)]
    all_gather x1, waiting for transfers between devices: 10 us -> 0.01 us  [per_device(): relay_z = lax.all_gather(z_own, 'fsdp', axis=0, tiled=True)]
  transfers between devices with their start and end apart: 10 -> 10, of which waited for: 8 -> 6; matrix products, arithmetic and copies ran while one was open for 24% -> 27% of each run, Pallas kernels for 0% -> 0%
where the time goes in v3:
time: 455 us; the launch traced here: 451 us
  waiting for transfers between devices  136 us (30%)
  blocking collectives  135 us (30%)
  other arithmetic  61.9 us (14%)
  local copies, waits for them, and re-layouts  40.4 us (9%)
  matrix products  35.2 us (8%)
  starting transfers between devices  28.6 us (6%)
  between operations  14.5 us (3%)
    all_to_all x6, waiting for transfers between devices, exchange(): lax.all_to_all(row_major(block), axis, split_axis=0, concat_axis=0, tiled...  136 us
    all_to_all x2, blocking collectives, exchange(): lax.all_to_all(row_major(block), axis, split_axis=0, concat_axis=0, tiled...  121 us
    all_to_all x6, starting transfers between devices, exchange(): lax.all_to_all(row_major(block), axis, split_axis=0, concat_axis=0, tiled...  28.3 us
    sub x2, other arithmetic, adam_update(): return master - learn_rate * (update + weight_decay * master)  20.1 us
    reduce_sum x1, other arithmetic, per_device(): sums.append(jnp.sum(c_mat[:, :, None] * state, axis=1) + d_skip * act_real)  15.2 us
    all_gather x1, blocking collectives, pick_rows(): every = lax.all_gather(mine, 'fsdp', axis=0, tiled=False)  13.6 us
    gather x1, local copies, waits for them, and re-layouts, pick_rows(): return embed_table.at[slots.reshape(-1)].get(mode='clip')  13.1 us
    dot_general x1, matrix products, per_device(): jnp.dot(normed, relay_z, preferred_element_type=jnp.float32)  10.1 us
  transfers between devices with their start and end apart: 10, of which 6 were waited for; matrix products, arithmetic and copies ran while one was open for 27% of the time, Pallas kernels for 0%

profile of v3, /device:TPU:0, one launch (start us, length us, event | category | flops | bytes accessed | tf_op | source)
XLA Modules:
  0.0 451.4 jit_solution(10642575767304607535)
XLA Ops:
  7.2 4.9 %fusion.14 = f32[128,4096]{1,0:T(8,128)S(1)} fusion(f32[128,4096]{1,0:T(8,128)} %param.23, bf16[128,4096]{1,0:T(8,128)(2,1)} %param.26, f32[128,4096]{1,0:T(8,128)} %param.25, f32[128,4096]{1,0:T(8,128)} %param.24), kind=kLoop, calls=%fused_computation.35 | loop fusion | flops 8388608 | bytes 9437184 | tf_op jit(solution)/shard_map/sub | solution.py:28
  14.7 5.2 %all-to-all-start = ((bf16[4,128,1024]{2,1,0:T(8,128)(2,1)}), bf16[4,128,1024]{2,1,0:T(8,128)(2,1)S(1)}, u32[]{:S(2)}, u32[]{:S(2)}) async-start(bf16[4,128,1024]{2,1,0:T(8,128)(2,1)} %pad_maximum_fusion.2), calls=%async_computation | async-start | bytes 2097152 | tf_op jit(solution)/shard_map/all_to_all | solution.py:37
  19.9 13.6 %all-to-all-done = bf16[4,128,1024]{2,1,0:T(8,128)(2,1)S(1)} async-done(((bf16[4,128,1024]{2,1,0:T(8,128)(2,1)}), bf16[4,128,1024]{2,1,0:T(8,128)(2,1)S(1)}, u32[]{:S(2)}, u32[]{:S(2)}) %all-to-all-start) | async-done | bytes 1048608 | tf_op jit(solution)/shard_map/all_to_all | solution.py:37
  33.5 13.6 %all-gather = s32[8,1,512]{2,1,0:T(1,128)S(1)} all-gather(s32[1,1,512]{2,1,0:T(1,128)S(1)} %bitcast.165), channel_id=1, replica_groups=mesh['fsdp'=8,'chan'=4] {'fsdp'}, dimensions={0}, use_global_device_ids=true | all-gather | bytes 18432 | tf_op jit(solution)/shard_map/all_gather | solution.py:65
  48.7 13.1 %gather_fusion = bf16[1024,1024]{1,0:T(8,128)(2,1)S(1)} fusion(bf16[8192,1024]{1,0:T(8,128)(2,1)} %param.27, s32[1024]{0:T(1024)S(1)} %broadcast_clamp_fusion), kind=kCustom, calls=%fused_computation | custom fusion | bytes 4198400 | tf_op jit(solution)/shard_map/gather | solution.py:72
  61.8 15.2 %multiply_subtract_fusion = f32[128,2,4096]{2,1,0:T(2,128)S(1)} fusion(f32[128,2,4096]{2,1,0:T(2,128)} %param.19, f32[128,2,4096]{2,1,0:T(2,128)} %param.21, bf16[128,2,4096]{2,1,0:T(2,128)(2,1)} %param.22, f32[128,2,4096]{2,1,0:T(2,128)} %param.20), kind=kLoop, calls=%fused_computation.25 | loop fusion | flops 16777216 | bytes 18874368 | tf_op jit(solution)/shard_map/sub | solution.py:28
  77.1 4.5 %fusion.90 = (bf16[128,1,4096]{2,1,0:T(2,128)(2,1)S(1)}, bf16[128,1,4096]{2,1,0:T(2,128)(2,1)S(1)}) fusion(f32[128,2,4096]{2,1,0:T(2,128)S(1)} %multiply_subtract_fusion), kind=kLoop, calls=%fused_computation.199 | loop fusion | bytes 4194304 | tf_op jit(solution)/shard_map/slice | solution.py:132
  86.1 4.3 all-to-all-start.2
  92.8 12.0 %all-to-all-done.2 = bf16[4,128,1024]{2,1,0:T(8,128)(2,1)} async-done(((bf16[4,128,1024]{2,1,0:T(8,128)(2,1)}), bf16[4,128,1024]{2,1,0:T(8,128)(2,1)}, u32[]{:S(2)}, u32[]{:S(2)}) %all-to-all-start.2) | async-done | bytes 1048608 | tf_op jit(solution)/shard_map/all_to_all | solution.py:37
  104.9 104.0 %all_to_all.47 = bf16[8,128,1024]{2,1,0:T(8,128)(2,1)} all-to-all(bf16[8,128,1024]{2,1,0:T(8,128)(2,1)S(1)} %bitcast.139), channel_id=1, replica_groups=mesh['fsdp'=8,'chan'=4] {'fsdp'}, dimensions={0} | all-to-all | bytes 4194304 | tf_op jit(solution)/shard_map/all_to_all | solution.py:37
  208.9 17.0 %all_to_all.48 = bf16[4,128,1024]{2,1,0:T(8,128)(2,1)} all-to-all(bf16[4,128,1024]{2,1,0:T(8,128)(2,1)S(1)} %copy-done.4), channel_id=1, replica_groups=mesh['fsdp'=8,'chan'=4] {'chan'}, dimensions={0} | all-to-all | bytes 2097152 | tf_op jit(solution)/shard_map/all_to_all | solution.py:37
  231.6 5.1 %all-to-all-start.4 = ((bf16[4,512,1024]{2,1,0:T(8,128)(2,1)}), bf16[4,512,1024]{2,1,0:T(8,128)(2,1)}, u32[]{:S(2)}, u32[]{:S(2)}) async-start(bf16[4,512,1024]{2,1,0:T(8,128)(2,1)} %broadcast_in_dim.28), calls=%async_computation.4 | async-start | bytes 8388608 | tf_op jit(solution)/shard_map/all_to_all | solution.py:37
  236.8 45.6 %all-to-all-done.4 = bf16[4,512,1024]{2,1,0:T(8,128)(2,1)} async-done(((bf16[4,512,1024]{2,1,0:T(8,128)(2,1)}), bf16[4,512,1024]{2,1,0:T(8,128)(2,1)}, u32[]{:S(2)}, u32[]{:S(2)}) %all-to-all-start.4) | async-done | bytes 4194336 | tf_op jit(solution)/shard_map/all_to_all | solution.py:37
  285.5 5.7 %fusion.8 = bf16[512,4,1024]{2,0,1:T(8,128)(2,1)} fusion(bf16[4,512,1024]{2,1,0:T(8,128)(2,1)} %all-to-all-done.4, f32[512]{0:T(512)S(1)} %add_rsqrt_fusion), kind=kLoop, calls=%fused_computation.22 | loop fusion | flops 6291456 | bytes 8390656 | tf_op jit(solution)/shard_map/transpose | solution.py:153
  291.2 6.3 %copy.41 = bf16[512,4,1024]{0,2,1:T(8,128)(2,1)} copy(bf16[512,4,1024]{2,0,1:T(8,128)(2,1)} %fusion.8) | data formatting | bytes 8388608 | tf_op jit(solution)/shard_map/transpose | solution.py:153
  297.5 9.2 %convolution_convert_fusion.1 = bf16[512,1024]{1,0:T(8,128)(2,1)S(1)} fusion(bf16[512,4096]{0,1:T(8,128)(2,1)} %bitcast.140, bf16[4096,1024]{1,0:T(8,128)(2,1)} %all-gather.8.cloned.1.call-done), kind=kOutput, calls=%fused_computation.56 | convolution fusion | flops 4295491584 | bytes 13631488 | tf_op jit(solution)/shard_map/dot_general | solution.py:155
  310.2 4.6 %all-to-all-start.5 = ((f32[4,512,288]{1,2,0:T(8,128)}), f32[4,512,288]{1,2,0:T(8,128)}, u32[]{:S(2)}, u32[]{:S(2)}) async-start(f32[4,512,288]{1,2,0:T(8,128)} %broadcast_in_dim.29.clone), calls=%async_computation.5 | async-start | bytes 4718592 | tf_op jit(solution)/shard_map/all_to_all | solution.py:37
  315.3 26.6 %all-to-all-done.5 = f32[4,512,288]{1,2,0:T(8,128)} async-done(((f32[4,512,288]{1,2,0:T(8,128)}), f32[4,512,288]{1,2,0:T(8,128)}, u32[]{:S(2)}, u32[]{:S(2)}) %all-to-all-start.5) | async-done | bytes 2359328 | tf_op jit(solution)/shard_map/all_to_all | solution.py:37
  351.5 15.2 %multiply_reduce_fusion.2 = (f32[128,1024]{1,0:T(8,128)S(1)}, f32[128,1024]{1,0:T(8,128)S(1)}, f32[128,1024]{1,0:T(8,128)S(1)}, f32[128,1024]{1,0:T(8,128)S(1)}, f32[128,16,1024]{2,1,0:T(8,128)}) fusion(f32[128,16]{1,0:T(8,128)S(1)} %get-tuple-element.73, f32[128,16]{1,0:T(8,128)S(1)} %get-tuple-element.72, f32[128,1024]{1,0:T(8,128)S(1)} %get-tuple-element.40, ...), kind=kLoop, calls=%fused_computation.9 | loop fusion | flops 49807360 | bytes 23199744 | tf_op jit(solution)/shard_map/reduce_sum | solution.py:195
  368.4 10.1 %fusion.24 = bf16[512,1024]{1,0:T(8,128)(2,1)S(1)} fusion(f32[128,1024]{1,0:T(8,128)} %get-tuple-element.82, f32[128,1024]{1,0:T(8,128)} %get-tuple-element.81, f32[128,1024]{1,0:T(8,128)} %get-tuple-element.80, f32[128,1024]{1,0:T(8,128)} %get-tuple-element.79, bf16[512,4096]{0,1:T(8,128)(2,1)} %bitcast.141, ...), kind=kOutput, calls=%fused_computation.53 | convolution fusion | flops 4300734464 | bytes 15728640 | tf_op jit(solution)/shard_map/dot_general | solution.py:197
  383.1 4.7 %all-to-all-start.6 = ((bf16[4,512,512]{2,1,0:T(8,128)(2,1)}), bf16[4,512,512]{2,1,0:T(8,128)(2,1)}, u32[]{:S(2)}, u32[]{:S(2)}) async-start(bf16[4,512,512]{2,1,0:T(8,128)(2,1)} %pad_maximum_fusion), calls=%async_computation.6 | async-start | bytes 4194304 | tf_op jit(solution)/shard_map/all_to_all | solution.py:37
  395.7 16.6 %all-to-all-done.6 = bf16[4,512,512]{2,1,0:T(8,128)(2,1)} async-done(((bf16[4,512,512]{2,1,0:T(8,128)(2,1)}), bf16[4,512,512]{2,1,0:T(8,128)(2,1)}, u32[]{:S(2)}, u32[]{:S(2)}) %all-to-all-start.6) | async-done | bytes 2097184 | tf_op jit(solution)/shard_map/all_to_all | solution.py:37
  412.3 4.5 all-to-all-start.7
  419.8 21.5 %all-to-all-done.7 = bf16[4,512,512]{2,1,0:T(8,128)(2,1)} async-done(((bf16[4,512,512]{2,1,0:T(8,128)(2,1)}), bf16[4,512,512]{2,1,0:T(8,128)(2,1)}, u32[]{:S(2)}, u32[]{:S(2)}) %all-to-all-start.7) | async-done | bytes 2097184 | tf_op jit(solution)/shard_map/all_to_all | solution.py:37
  (98 shorter events, 54.0 us)
Async XLA Ops:
  7.2 300.7 %copy-start = (bf16[288,1024]{1,0:T(8,128)(2,1)S(1)}, bf16[288,1024]{1,0:T(8,128)(2,1)}, u32[]{:S(2)}) copy-start(bf16[288,1024]{1,0:T(8,128)(2,1)} %param.33) | copy-start | bytes 1769476
  13.4 20.2 %copy-start.9 = (s32[4,128]{1,0:T(4,128)S(1)}, s32[4,128]{1,0:T(4,128)}, u32[]{:S(2)}) copy-start(s32[4,128]{1,0:T(4,128)} %param.28) | copy-start | bytes 6148
  14.7 18.8 %all-to-all-start = ((bf16[4,128,1024]{2,1,0:T(8,128)(2,1)}), bf16[4,128,1024]{2,1,0:T(8,128)(2,1)S(1)}, u32[]{:S(2)}, u32[]{:S(2)}) async-start(bf16[4,128,1024]{2,1,0:T(8,128)(2,1)} %pad_maximum_fusion.2), calls=%async_computation | async-start | bytes 2097152 | tf_op jit(solution)/shard_map/all_to_all | solution.py:37
  19.9 84.9 %all-gather.6.cloned.1.call-start = ((), (), s32[]{:S(2)}) async-start(), calls=%async_computation.8 | async-start | bytes 4718592 | tf_op jit(solution)/shard_map/all_gather | solution.py:137
  77.1 4.6 %copy-start.2 = (f32[128,2,4096]{2,1,0:T(2,128)}, f32[128,2,4096]{2,1,0:T(2,128)S(1)}, u32[]{:S(2)}) copy-start(f32[128,2,4096]{2,1,0:T(2,128)S(1)} %multiply_subtract_fusion) | copy-start | bytes 12582916
  86.1 18.7 %all-to-all-start.2 = ((bf16[4,128,1024]{2,1,0:T(8,128)(2,1)}), bf16[4,128,1024]{2,1,0:T(8,128)(2,1)}, u32[]{:S(2)}, u32[]{:S(2)}) async-start(bf16[4,128,1024]{2,1,0:T(8,128)(2,1)} %pad_maximum_fusion.4), calls=%async_computation.2 | async-start | bytes 2097152 | tf_op jit(solution)/shard_map/all_to_all | solution.py:37
  90.4 207.2 %all-gather.8.cloned.1.call-start = ((), (), s32[]{:S(2)}) async-start(), calls=%async_computation.9 | async-start | bytes 9437184 | tf_op jit(solution)/shard_map/all_gather | solution.py:139
  104.8 263.6 %all-gather.10.cloned.1.call-start = ((), (), s32[]{:S(2)}) async-start(), calls=%async_computation.10 | async-start | bytes 9437184 | tf_op jit(solution)/shard_map/all_gather | solution.py:142
  104.9 104.0 %copy-start.4 = (bf16[4,128,1024]{2,1,0:T(8,128)(2,1)S(1)}, bf16[4,128,1024]{2,1,0:T(8,128)(2,1)}, u32[]{:S(2)}) copy-start(bf16[4,128,1024]{2,1,0:T(8,128)(2,1)} %pad_maximum_fusion.3) | copy-start | bytes 3145732
  231.6 5.1 %copy-start.10 = (f32[4,1024]{1,0:T(4,128)S(1)}, f32[4,1024]{1,0:T(4,128)}, u32[]{:S(2)}) copy-start(f32[4,1024]{1,0:T(4,128)} %param.31) | copy-start | bytes 49156
  231.6 50.8 %all-to-all-start.4 = ((bf16[4,512,1024]{2,1,0:T(8,128)(2,1)}), bf16[4,512,1024]{2,1,0:T(8,128)(2,1)}, u32[]{:S(2)}, u32[]{:S(2)}) async-start(bf16[4,512,1024]{2,1,0:T(8,128)(2,1)} %broadcast_in_dim.28), calls=%async_computation.4 | async-start | bytes 8388608 | tf_op jit(solution)/shard_map/all_to_all | solution.py:37
  297.5 9.2 %copy-start.6 = (f32[1024]{0:T(1024)S(1)}, f32[1024]{0:T(1024)}, u32[]{:S(2)}) copy-start(f32[1024]{0:T(1024)} %param.32) | copy-start | bytes 12292
  297.5 9.6 %copy-start.5 = (bf16[128,3,1024]{2,0,1:T(8,128)(2,1)S(1)}, bf16[128,3,1024]{2,0,1:T(8,128)(2,1)}, u32[]{:S(2)}) copy-start(bf16[128,3,1024]{2,0,1:T(8,128)(2,1)} %param.29) | copy-start | bytes 2359300
  308.4 6.9 %copy-start.8 = (f32[16,1024]{1,0:T(8,128)S(1)}, f32[16,1024]{1,0:T(8,128)}, u32[]{:S(2)}) copy-start(f32[16,1024]{1,0:T(8,128)} %param.36) | copy-start | bytes 196612
  310.2 31.8 %all-to-all-start.5 = ((f32[4,512,288]{1,2,0:T(8,128)}), f32[4,512,288]{1,2,0:T(8,128)}, u32[]{:S(2)}, u32[]{:S(2)}) async-start(f32[4,512,288]{1,2,0:T(8,128)} %broadcast_in_dim.29.clone), calls=%async_computation.5 | async-start | bytes 4718592 | tf_op jit(solution)/shard_map/all_to_all | solution.py:37
  314.7 73.1 %all-gather.12.cloned.1.call-start = ((), (), s32[]{:S(2)}) async-start(), calls=%async_computation.11 | async-start | bytes 4718592 | tf_op jit(solution)/shard_map/all_gather | solution.py:144
  345.1 4.9 %slice-start = ((s8[8388608]{0:T(1024)(128)(4,1)}), s8[4194304]{0:T(1024)(128)(4,1)S(1)}, s32[]{:S(2)}) async-start(s8[8388608]{0:T(1024)(128)(4,1)} %bitcast.137), calls=%async_computation.12 | async-start | bytes 8388608
  351.5 15.2 %copy-start.11 = (f32[1024]{0:T(1024)S(1)}, f32[1024]{0:T(1024)}, u32[]{:S(2)}) copy-start(f32[1024]{0:T(1024)} %param.37) | copy-start | bytes 12292
  368.4 10.1 %copy-start.12 = (bf16[2048,1024]{1,0:T(8,128)(2,1)S(1)}, bf16[2048,1024]{1,0:T(8,128)(2,1)}, u32[]{:S(2)}) copy-start(bf16[2048,1024]{1,0:T(8,128)(2,1)} %all-gather.6.cloned.1.call-done) | copy-start | bytes 12582916
  383.1 29.2 %all-to-all-start.6 = ((bf16[4,512,512]{2,1,0:T(8,128)(2,1)}), bf16[4,512,512]{2,1,0:T(8,128)(2,1)}, u32[]{:S(2)}, u32[]{:S(2)}) async-start(bf16[4,512,512]{2,1,0:T(8,128)(2,1)} %pad_maximum_fusion), calls=%async_computation.6 | async-start | bytes 4194304 | tf_op jit(solution)/shard_map/all_to_all | solution.py:37
  387.8 4.8 %copy-start.13 = (bf16[2048,1024]{1,0:T(8,128)(2,1)S(1)}, bf16[2048,1024]{1,0:T(8,128)(2,1)}, u32[]{:S(2)}) copy-start(bf16[2048,1024]{1,0:T(8,128)(2,1)} %all-gather.12.cloned.1.call-done) | copy-start | bytes 12582916
  387.8 4.8 %copy-start.15 = (bf16[512,1024]{1,0:T(8,128)(2,1)S(1)}, bf16[512,1024]{1,0:T(8,128)(2,1)}, u32[]{:S(2)}) copy-start(bf16[512,1024]{1,0:T(8,128)(2,1)} %copy-done.14) | copy-start | bytes 3145732
  412.3 29.0 %all-to-all-start.7 = ((bf16[4,512,512]{2,1,0:T(8,128)(2,1)}), bf16[4,512,512]{2,1,0:T(8,128)(2,1)}, u32[]{:S(2)}, u32[]{:S(2)}) async-start(bf16[4,512,512]{2,1,0:T(8,128)(2,1)} %pad_maximum_fusion.1), calls=%async_computation.7 | async-start | bytes 4194304 | tf_op jit(solution)/shard_map/all_to_all | solution.py:37
  419.7 24.9 %copy-start.1 = (bf16[288,1024]{1,0:T(8,128)(2,1)S(1)}, bf16[288,1024]{1,0:T(8,128)(2,1)}, u32[]{:S(2)}) copy-start(bf16[288,1024]{1,0:T(8,128)(2,1)} %param.33) | copy-start | bytes 1769476
  (4 other events, 10.0 us)
Sparse Core Ops, SparseCore 0:
  48.3 45.6 all-gather.5
  105.0 121.1 all-gather.7
  227.8 80.0 all-gather.9
  316.8 48.5 all-gather.11
